TPU v7x, 32 devices: a whole 2x2x4 slice. The times are simulated.
32 devices in a mesh: lat: 8 (over y, x, core), depth: 4 (over z).
Axes of the slice: x: 2, y: 2, z: 4, core: 2. Of those that a mesh axis runs over, the one named last changes fastest.
Arguments:
- velocity_fine: float32 [3, 96, 64, 384], P(None, 'lat', 'depth'), may hold values from -6 to 6
- stress_fine: float32 [6, 96, 64, 384], P(None, 'lat', 'depth'), may hold values from -6 to 6
- memory_fine: float32 [6, 96, 64, 384], P(None, 'lat', 'depth'), may hold values from -1.8 to 1.8
- peak_fine: float32 [96, 64, 384], P('lat', 'depth'), may hold values from 0 to 12
- zone_fine: int32 [96, 64, 384], P('lat', 'depth'), may hold values from 0 to 7
- velocity_coarse: float32 [3, 32, 128, 128], P(None, 'lat', 'depth'), may hold values from -6 to 6
- stress_coarse: float32 [6, 32, 128, 128], P(None, 'lat', 'depth'), may hold values from -6 to 6
- memory_coarse: float32 [6, 32, 128, 128], P(None, 'lat', 'depth'), may hold values from -1.8 to 1.8
- peak_coarse: float32 [32, 128, 128], P('lat', 'depth'), may hold values from 0 to 12
- zone_coarse: int32 [32, 128, 128], P('lat', 'depth'), may hold values from 0 to 7
- zone_table: float32 [8, 5], replicated, may hold values from 0.05 to 1, as said below
- interp_weight: int32 [2, 3], replicated, may hold values from 0 to 8
- restrict_weight: int32 [2, 3], replicated, may hold values from 1 to 8
Outputs:
- fine_velocity: float32 [3, 96, 64, 384], P(None, 'lat', 'depth')
- fine_stress: float32 [6, 96, 64, 384], P(None, 'lat', 'depth')
- fine_memory: float32 [6, 96, 64, 384], P(None, 'lat', 'depth')
- fine_peak: float32 [96, 64, 384], P('lat', 'depth')
- coarse_velocity: float32 [3, 32, 128, 128], P(None, 'lat', 'depth')
- coarse_stress: float32 [6, 32, 128, 128], P(None, 'lat', 'depth')
- coarse_memory: float32 [6, 32, 128, 128], P(None, 'lat', 'depth')
- coarse_peak: float32 [32, 128, 128], P('lat', 'depth')
Inputs may be any that keep to these rules, and one draw needn't show every extreme that they name: `zone_table`: column 0 lies in 0.5 to 1, columns 1 and 2 in 0.1 to 0.3, column 3 in 0.5 to 0.95, column 4 in 0.05 to 0.3.
All inputs are finite; a program needn't handle non-finite values.
Results may differ from a plain program's by a relative error of at most 0.0003.
Values sent between devices are 32-bit elements; how exact they have to be, the bound alone decides.
A program may use at most 128 MiB of HBM per device.

v0:
```python
import jax
import jax.numpy as jnp
from jax import lax
from jax.experimental import pallas as pl
from jax.experimental.pallas import tpu as pltpu
from jax.sharding import PartitionSpec as P

STEPS = 2


time_step = 0.4
near_coef = 9.0 / 8.0
far_coef = 1.0 / 24.0


def derivative(field, low, high, dim):
    wide = jnp.concatenate([low, field, high], axis=dim)
    count = field.shape[dim]

    def at(begin):
        return lax.slice_in_dim(wide, begin, begin + count, axis=dim)

    return near_coef * (at(2) - at(1)) - far_coef * (at(3) - at(0))


FORWARD = (1, 2)
BACKWARD = (2, 1)


def derivative_y(field, kind):
    wide = jnp.pad(field, ((0, 0), (0, 0), kind))
    count = field.shape[2]

    def at(begin):
        return lax.slice_in_dim(wide, begin, begin + count, axis=2)

    return near_coef * (at(2) - at(1)) - far_coef * (at(3) - at(0))


def materials_kernel(table_ref, zone_ref, *column_refs):

    def row(index, carry):
        zone = zone_ref[index]
        masks = [zone == level for level in range(1, table_ref.shape[0])]
        for column, ref in enumerate(column_refs):
            value = jnp.full(zone.shape, table_ref[0, column], jnp.float32)
            for level, mask in enumerate(masks):
                value = jnp.where(mask, table_ref[level + 1, column], value)
            ref[index] = value
        return carry

    lax.fori_loop(0, zone_ref.shape[0], row, 0)


def materials(zone, zone_table):
    whole = pl.BlockSpec(memory_space=pltpu.VMEM)
    return pl.pallas_call(
        materials_kernel,
        out_shape=[jax.ShapeDtypeStruct(zone.shape, jnp.float32)] * 5,
        in_specs=[pl.BlockSpec(memory_space=pltpu.SMEM), whole],
        out_specs=[whole] * 5,
    )(zone_table, zone)


STRESS_X = ((0, FORWARD), (3, BACKWARD), (4, BACKWARD))
STRESS_Z = ((4, BACKWARD), (5, BACKWARD), (2, FORWARD))
VELOCITY_X = ((0, BACKWARD), (1, FORWARD), (2, FORWARD))
VELOCITY_Z = ((0, FORWARD), (1, FORWARD), (2, BACKWARD))


def velocity_update(stress, velocity, buoyancy, spacing, ghosts):
    low_x, high_x, low_z, high_z = ghosts

    def along_x(slot):
        return derivative(stress[STRESS_X[slot][0]], low_x[slot], high_x[slot], 0)

    def along_z(slot):
        return derivative(stress[STRESS_Z[slot][0]], low_z[slot], high_z[slot], 1)

    accel_x = along_x(0) + derivative_y(stress[3], BACKWARD) + along_z(0)
    accel_y = along_x(1) + derivative_y(stress[1], FORWARD) + along_z(1)
    accel_z = along_x(2) + derivative_y(stress[5], BACKWARD) + along_z(2)
    accel = jnp.stack([accel_x, accel_y, accel_z])
    return velocity + time_step / spacing * buoyancy[None] * accel


def stress_update(velocity, stress, memory, props, spacing, ghosts):
    lame, shear, decay, damping = props[1:]
    low_x, high_x, low_z, high_z = ghosts

    def along_x(part):
        return derivative(velocity[part], low_x[part], high_x[part], 0)

    def along_z(part):
        return derivative(velocity[part], low_z[part], high_z[part], 1)

    normal_x = along_x(0)
    normal_y = derivative_y(velocity[1], BACKWARD)
    normal_z = along_z(2)
    shear_xy = 0.5 * (derivative_y(velocity[0], FORWARD) + along_x(1))
    shear_xz = 0.5 * (along_z(0) + along_x(2))
    shear_yz = 0.5 * (along_z(1) + derivative_y(velocity[2], FORWARD))
    volume = normal_x + normal_y + normal_z
    rate = (
        jnp.stack(
            [
                lame * volume + 2.0 * shear * normal_x,
                lame * volume + 2.0 * shear * normal_y,
                lame * volume + 2.0 * shear * normal_z,
                2.0 * shear * shear_xy,
                2.0 * shear * shear_xz,
                2.0 * shear * shear_yz,
            ]
        )
        / spacing
    )
    memory_next = decay[None] * memory - (damping * (1.0 - decay))[None] * rate
    stress_next = stress + time_step * (rate + 0.5 * (memory + memory_next))
    return (stress_next, memory_next)


def entry_key(first, second):
    return (min(first, second), max(first, second))


def rotate(entries, first, second):
    other = 3 - first - second
    pivot = entries[first, second]
    gap = entries[second, second] - entries[first, first]
    denominator = jnp.abs(gap) + jnp.sqrt(gap * gap + 4.0 * pivot * pivot)
    direction = jnp.where(gap >= 0, 1.0, -1.0)
    usable = denominator > 0
    tangent = jnp.where(usable, 2.0 * pivot * direction / jnp.where(usable, denominator, 1.0), 0.0)
    cosine = 1.0 / jnp.sqrt(1.0 + tangent * tangent)
    sine = tangent * cosine
    low_entry = entries[entry_key(other, first)]
    high_entry = entries[entry_key(other, second)]
    result = dict(entries)
    result[first, first] = entries[first, first] - tangent * pivot
    result[second, second] = entries[second, second] + tangent * pivot
    result[first, second] = jnp.zeros_like(pivot)
    result[entry_key(other, first)] = cosine * low_entry - sine * high_entry
    result[entry_key(other, second)] = sine * low_entry + cosine * high_entry
    return result


def strain_peak(stress, props, peak):
    lame, shear = (props[1], props[2])
    trace = stress[0] + stress[1] + stress[2]
    isotropic = lame * trace / (3.0 * lame + 2.0 * shear)
    scale = 0.5 / shear
    entries = {
        (0, 0): (stress[0] - isotropic) * scale,
        (1, 1): (stress[1] - isotropic) * scale,
        (2, 2): (stress[2] - isotropic) * scale,
        (0, 1): stress[3] * scale,
        (0, 2): stress[4] * scale,
        (1, 2): stress[5] * scale,
    }
    for sweep in range(3):
        entries = rotate(entries, 0, 1)
        entries = rotate(entries, 0, 2)
        entries = rotate(entries, 1, 2)
    principal = jnp.maximum(jnp.maximum(entries[0, 0], entries[1, 1]), entries[2, 2])
    return jnp.maximum(peak, principal)


def make_tables(interp_weight, restrict_weight, coarse_cells):
    x_share = interp_weight[0].astype(jnp.float32) / 8.0
    y_share = interp_weight[1].astype(jnp.float32) / 8.0
    x_weight = restrict_weight[0].astype(jnp.float32)
    y_weight = restrict_weight[1].astype(jnp.float32)
    coarse_index = lax.broadcasted_iota(jnp.int32, (coarse_cells, 3 * coarse_cells), 0)
    fine_index = lax.broadcasted_iota(jnp.int32, (coarse_cells, 3 * coarse_cells), 1)
    phase = fine_index % 3
    block = fine_index // 3
    y_interp = jnp.where(phase == 0, y_share[0], jnp.where(phase == 1, y_share[1], y_share[2]))
    y_restrict = jnp.where(phase == 0, y_weight[0], jnp.where(phase == 1, y_weight[1], y_weight[2]))
    y_spread = jnp.where(coarse_index == block, y_interp, 0.0) + jnp.where(
        coarse_index == block + 1, 1.0 - y_interp, 0.0
    )
    y_gather = jnp.where(coarse_index == block, y_restrict, 0.0).T
    normaliser = 3.0 * jnp.sum(x_weight) * jnp.sum(y_weight)
    return (x_share, y_spread, x_weight, y_gather, normaliser)


def interpolate(planes, tables):
    x_share, y_spread = (tables[0], tables[1])
    upper = planes[:, :, 0:1]
    lower = planes[:, :, 1:2]
    layered = jnp.concatenate([(2.0 * upper + lower) / 3.0, (upper + 2.0 * lower) / 3.0], axis=2)
    share = x_share[None, None, :, None, None]
    across = share * layered[:, :-1, None] + (1.0 - share) * layered[:, 1:, None]
    count, rows = (across.shape[0], across.shape[1])
    flat = across.reshape(count * rows * 6, -1)
    spread = jnp.dot(flat, y_spread, precision=lax.Precision.HIGHEST)
    return spread.reshape(count, rows * 3, 2, -1)


def restrict(block, tables):
    x_weight, y_gather, normaliser = (tables[2], tables[3], tables[4])
    count, rows = (block.shape[0], block.shape[1])
    layers = jnp.sum(block.reshape(count, rows, 2, 3, -1), axis=3)
    grouped = layers.reshape(count, rows // 3, 3, 2, -1)
    across = jnp.sum(x_weight[None, None, :, None, None] * grouped, axis=2)
    flat = across.reshape(count * (rows // 3) * 2, -1)
    gathered = jnp.dot(flat, y_gather, precision=lax.Precision.HIGHEST)
    return gathered.reshape(count, rows // 3, 2, -1) / normaliser


def lane_slabs(block, width, dim):
    count = block.shape[-1] // width
    slabs = [block[..., i * width : (i + 1) * width] for i in range(count)]
    return jnp.concatenate(slabs, axis=dim)


def lane_joined(block, count, dim):
    return jnp.concatenate(jnp.split(block, count, axis=dim), axis=-1)


def lateral_message(fine, coarse):
    folds = coarse.shape[1] // fine.shape[1]
    return jnp.concatenate([fine, lane_joined(coarse, folds, 1)], axis=-1)


def cut_rows(block, kinds, side):
    parts = []
    begin = 0
    for _, kind in kinds:
        parts.append(block[begin : begin + kind[side]])
        begin += kind[side]
    return parts


def exchange(fine, coarse, along_x, along_z, tables):
    lats = lax.axis_size("lat")
    depths = lax.axis_size("depth")
    depth_index = lax.axis_index("depth")

    def low_rows(field):
        return jnp.concatenate([field[part, -kind[0] :] for part, kind in along_x], axis=0)

    def high_rows(field):
        return jnp.concatenate([field[part, : kind[1]] for part, kind in along_x], axis=0)

    def layers(field, begin, end):
        return jnp.stack([field[part, :, begin:end] for part, _ in along_z])

    from_below = lax.ppermute(
        lateral_message(low_rows(fine), low_rows(coarse)),
        "lat",
        [(i, i + 1) for i in range(lats - 1)],
    )
    from_above = lax.ppermute(
        lateral_message(high_rows(fine), high_rows(coarse)),
        "lat",
        [(i + 1, i) for i in range(lats - 1)],
    )
    width = coarse.shape[3]
    folds = fine.shape[3] // width
    split = fine.shape[1] * folds
    coarse_head = layers(coarse, 0, 2)
    head = jnp.concatenate([lane_slabs(layers(fine, 0, 2), width, 1), coarse_head], axis=1)
    from_next = lax.ppermute(head, "depth", [((i + 1) % depths, i) for i in range(depths)])
    corner = lax.ppermute(
        coarse_head[:, :1],
        ("lat", "depth"),
        [((i + 1) * depths, i * depths + depths - 1) for i in range(lats - 1)],
    )
    size = fine.shape[2]
    lifted = restrict(layers(fine, size - 6, size), tables)
    deep = coarse.shape[2]
    coarse_tail = jnp.where(depth_index == depths - 1, lifted, layers(coarse, deep - 2, deep))
    tail = jnp.concatenate(
        [lane_slabs(layers(fine, size - 2, size), width, 1), coarse_tail], axis=1
    )
    from_previous = lax.ppermute(tail, "depth", [(i, (i + 1) % depths) for i in range(depths)])

    fine_below, coarse_below = (
        from_below[..., : fine.shape[3]],
        lane_slabs(from_below[..., fine.shape[3] :], width, 1),
    )
    fine_above, coarse_above = (
        from_above[..., : fine.shape[3]],
        lane_slabs(from_above[..., fine.shape[3] :], width, 1),
    )
    fine_low = jnp.where(depth_index == 0, 0.0, lane_joined(from_previous[:, :split], folds, 1))
    coarse_low = from_previous[:, split:]
    received = from_next[:, split:]
    ghost = interpolate(jnp.concatenate([received, corner], axis=1), tables)
    last = depth_index == depths - 1
    fine_high = jnp.where(last, ghost, lane_joined(from_next[:, :split], folds, 1))
    coarse_high = jnp.where(last, 0.0, received)

    def ghosts(below, above, low, high):
        return (
            cut_rows(below, along_x, 0),
            cut_rows(above, along_x, 1),
            [low[slot, :, 2 - kind[0] :] for slot, (_, kind) in enumerate(along_z)],
            [high[slot, :, : kind[1]] for slot, (_, kind) in enumerate(along_z)],
        )

    return (
        ghosts(fine_below, fine_above, fine_low, fine_high),
        ghosts(coarse_below, coarse_above, coarse_low, coarse_high),
    )


def on_device(
    velocity_fine,
    stress_fine,
    memory_fine,
    peak_fine,
    zone_fine,
    velocity_coarse,
    stress_coarse,
    memory_coarse,
    peak_coarse,
    zone_coarse,
    zone_table,
    interp_weight,
    restrict_weight,
):
    tables = make_tables(interp_weight, restrict_weight, stress_coarse.shape[3])
    props_fine = materials(zone_fine, zone_table)
    props_coarse = materials(zone_coarse, zone_table)
    for step in range(STEPS):
        fine_ghosts, coarse_ghosts = exchange(
            stress_fine, stress_coarse, STRESS_X, STRESS_Z, tables
        )
        velocity_fine = velocity_update(
            stress_fine, velocity_fine, props_fine[0], 1.0, fine_ghosts
        )
        velocity_coarse = velocity_update(
            stress_coarse, velocity_coarse, props_coarse[0], 3.0, coarse_ghosts
        )
        fine_ghosts, coarse_ghosts = exchange(
            velocity_fine, velocity_coarse, VELOCITY_X, VELOCITY_Z, tables
        )
        stress_fine, memory_fine = stress_update(
            velocity_fine, stress_fine, memory_fine, props_fine, 1.0, fine_ghosts
        )
        stress_coarse, memory_coarse = stress_update(
            velocity_coarse, stress_coarse, memory_coarse, props_coarse, 3.0, coarse_ghosts
        )
        peak_fine = strain_peak(stress_fine, props_fine, peak_fine)
        peak_coarse = strain_peak(stress_coarse, props_coarse, peak_coarse)
    return (
        velocity_fine,
        stress_fine,
        memory_fine,
        peak_fine,
        velocity_coarse,
        stress_coarse,
        memory_coarse,
        peak_coarse,
    )


def solution(mesh):
    in_specs = (
        P(None, "lat", "depth", None),
        P(None, "lat", "depth", None),
        P(None, "lat", "depth", None),
        P("lat", "depth", None),
        P("lat", "depth", None),
        P(None, "lat", "depth", None),
        P(None, "lat", "depth", None),
        P(None, "lat", "depth", None),
        P("lat", "depth", None),
        P("lat", "depth", None),
        P(),
        P(),
        P(),
    )
    out_specs = (
        P(None, "lat", "depth", None),
        P(None, "lat", "depth", None),
        P(None, "lat", "depth", None),
        P("lat", "depth", None),
        P(None, "lat", "depth", None),
        P(None, "lat", "depth", None),
        P(None, "lat", "depth", None),
        P("lat", "depth", None),
    )
    return jax.shard_map(
        on_device, mesh=mesh, in_specs=in_specs, out_specs=out_specs, check_vma=False
    )
```

profile of v0, /device:TPU:4, one launch (start us, length us, event | category | flops | bytes accessed | tf_op | source)
XLA Modules:
  0.0 180.3 jit_solution(10300637122317693063)
XLA Ops:
  2.9 5.8 %collective-permute-start.4 = (f32[3,1,2,128]{3,2,1,0:T(2,128)}, f32[3,1,2,128]{3,2,1,0:T(2,128)S(1)}, u32[]{:S(2)}, u32[]{:S(2)}) collective-permute-start(f32[3,1,2,128]{3,2,1,0:T(2,128)} %pad_maximum_fusion.127), channel_id=1, source_target_pairs={{4,3},{8,7},{12,11},{16,15},{20,19},{24,23},{28,27}} | collective-permute-start | bytes 9224 | tf_op jit(solution)/shard_map/ppermute | solution.py:265
  15.5 2.7 %collective-permute-start = (f32[4,16,640]{2,1,0:T(8,128)}, f32[4,16,640]{2,1,0:T(8,128)}, u32[]{:S(2)}, u32[]{:S(2)}) collective-permute-start(f32[4,16,640]{2,1,0:T(8,128)} %pad_maximum_fusion.54), channel_id=1, source_target_pairs={{4,0},{8,4},{12,8},{16,12},{20,16},{24,20},{28,24},{5,1},{9,5},{13... | collective-permute-start | bytes 491528 | tf_op jit(solution)/shard_map/ppermute | solution.py:254
  24.0 2.1 %fusion.3 = f32[3,4,2,128]{3,2,1,0:T(2,128)S(1)} fusion(f32[3,4,2,384]{3,2,1,0:T(2,128)S(1)} %multiply_reduce_fusion.3, f32[]{:T(128)} %bitcast.20, f32[]{:T(128)} %bitcast.19, f32[]{:T(128)} %bitcast.18, s32[384]{0:T(512)S(1)} %get-tuple-element.317, s32[384]{0:T(512)S(1)} %get-tuple-element.318, s32[384]{0:T(512)S(1)} %get-tuple-element.316, ...), kind=kOutput, calls=%fused_computation.11 | convolution fusion | flops 14558208 | bytes 68369 | tf_op jit(solution)/shard_map/dot_general | solution.py:207
  33.9 2.8 %shard_map.188 = (f32[12,16,384]{2,1,0:T(8,128)}, f32[12,16,384]{2,1,0:T(8,128)}, f32[12,16,384]{2,1,0:T(8,128)}, f32[12,16,384]{2,1,0:T(8,128)}, f32[12,16,384]{2,1,0:T(8,128)}) custom-call(f32[8,5]{1,0:T(8,128)} %table_ref.3, s32[12,16,384]{2,1,0:T(8,128)} %zone_ref.2), custom_call_target="tpu_custom_call" | custom-call | tf_op jit(solution)/shard_map/pallas_call | solution.py:57
  46.6 2.9 %fusion.371 = f32[3,12,2,384]{3,1,2,0:T(8,128)S(1)} fusion(f32[]{:T(128)} %bitcast.29, f32[]{:T(128)} %bitcast.28, f32[]{:T(128)} %bitcast.27, s32[384]{0:T(512)} %copy-done.77, s32[384]{0:T(512)} %copy-done.71, s32[384]{0:T(512)} %copy-done.75, s32[384]{0:T(512)} %copy-done.73, pred[384]{0:T(512)(128)(4,1)} %copy-done.84, pred[384]{0:T(512)(128)(4,1)} %copy-done.82, ...), kind=kOutput, calls=%fused_computation.746 | convolution fusion | flops 43106304 | bytes 154380 | tf_op jit(solution)/shard_map/dot_general | solution.py:196
  60.5 5.9 %collective-permute-start.9 = (f32[3,1,2,128]{3,2,1,0:T(2,128)S(1)}, f32[3,1,2,128]{3,2,1,0:T(2,128)S(1)}, u32[]{:S(2)}, u32[]{:S(2)}) collective-permute-start(f32[3,1,2,128]{3,2,1,0:T(2,128)S(1)} %slice.2533), channel_id=1, source_target_pairs={{4,3},{8,7},{12,11},{16,15},{20,19},{24,23},{28,27}} | collective-permute-start | bytes 9224 | tf_op jit(solution)/shard_map/ppermute | solution.py:265
  69.7 4.5 %collective-permute-start.6 = (f32[5,16,640]{2,1,0:T(8,128)}, f32[5,16,640]{2,1,0:T(8,128)}, u32[]{:S(2)}, u32[]{:S(2)}) collective-permute-start(f32[5,16,640]{2,1,0:T(8,128)} %pad_maximum_fusion.51), channel_id=1, source_target_pairs={{4,0},{8,4},{12,8},{16,12},{20,16},{24,20},{28,24},{5,1},{9,5},{13... | collective-permute-start | bytes 614408 | tf_op jit(solution)/shard_map/ppermute | solution.py:254
  77.2 2.8 %fusion.2 = f32[3,4,2,128]{3,2,1,0:T(2,128)S(1)} fusion(f32[3,4,2,384]{3,2,1,0:T(2,128)S(1)} %multiply_reduce_fusion.2, f32[]{:T(128)} %bitcast.20, f32[]{:T(128)} %bitcast.19, f32[]{:T(128)} %bitcast.18, s32[384]{0:T(512)} %copy-done.77, s32[384]{0:T(512)S(1)} %copy-done.72, s32[384]{0:T(512)} %copy-done.75, s32[384]{0:T(512)} %copy-done.73, ...), kind=kOutput, calls=%fused_computation.9 | convolution fusion | flops 14555136 | bytes 68369 | tf_op jit(solution)/shard_map/dot_general | solution.py:207
  80.0 2.1 %collective-permute-start.7 = (f32[3,40,2,128]{3,2,1,0:T(2,128)S(1)}, f32[3,40,2,128]{3,2,1,0:T(2,128)S(1)}, u32[]{:S(2)}, u32[]{:S(2)}) collective-permute-start(f32[3,40,2,128]{3,2,1,0:T(2,128)S(1)} %pad_maximum_fusion.62), channel_id=1, source_target_pairs={{0,1},{1,2},{2,3},{3,0},{4,5},{5,6},{6,7},{7,4},{8,9},{9,10},{10,1... | collective-permute-start | bytes 368648 | tf_op jit(solution)/shard_map/ppermute | solution.py:277
  83.2 2.8 %fusion.369 = f32[3,12,2,384]{3,1,2,0:T(8,128)S(1)} fusion(f32[]{:T(128)} %bitcast.29, f32[]{:T(128)} %bitcast.28, f32[]{:T(128)} %bitcast.27, s32[384]{0:T(512)S(1)} %copy-done.78, s32[384]{0:T(512)S(1)} %copy-done.72, s32[384]{0:T(512)S(1)} %copy-done.76, s32[384]{0:T(512)S(1)} %copy-done.74, pred[384]{0:T(512)(128)(4,1)} %copy-done.84, ...), kind=kOutput, calls=%fused_computation.745 | convolution fusion | flops 43106304 | bytes 154380 | tf_op jit(solution)/shard_map/dot_general | solution.py:196
  99.5 3.5 %collective-permute-start.14 = (f32[3,1,2,128]{3,2,1,0:T(2,128)}, f32[3,1,2,128]{3,2,1,0:T(2,128)}, u32[]{:S(2)}, u32[]{:S(2)}) collective-permute-start(f32[3,1,2,128]{3,2,1,0:T(2,128)} %pad_maximum_fusion.126), channel_id=1, source_target_pairs={{4,3},{8,7},{12,11},{16,15},{20,19},{24,23},{28,27}} | collective-permute-start | bytes 9224 | tf_op jit(solution)/shard_map/ppermute | solution.py:265
  107.0 2.8 %collective-permute-start.11 = (f32[5,16,640]{2,1,0:T(8,128)}, f32[5,16,640]{2,1,0:T(8,128)}, u32[]{:S(2)}, u32[]{:S(2)}) collective-permute-start(f32[5,16,640]{2,1,0:T(8,128)} %pad_maximum_fusion.52), channel_id=1, source_target_pairs={{0,4},{4,8},{8,12},{12,16},{16,20},{20,24},{24,28},{1,5},{5,9},{9,... | collective-permute-start | bytes 614408 | tf_op jit(solution)/shard_map/ppermute | solution.py:249
  113.6 2.8 %fusion.1 = f32[3,4,2,128]{3,2,1,0:T(2,128)S(1)} fusion(f32[3,4,2,384]{3,2,1,0:T(2,128)S(1)} %multiply_reduce_fusion.1, f32[]{:T(128)} %bitcast.20, f32[]{:T(128)} %bitcast.19, f32[]{:T(128)} %bitcast.18, s32[384]{0:T(512)} %copy-done.77, s32[384]{0:T(512)} %copy-done.71, s32[384]{0:T(512)} %copy-done.75, s32[384]{0:T(512)} %copy-done.73, ...), kind=kOutput, calls=%fused_computation.7 | convolution fusion | flops 14558208 | bytes 68369 | tf_op jit(solution)/shard_map/dot_general | solution.py:207
  116.5 2.0 %collective-permute-start.12 = (f32[3,40,2,128]{3,2,1,0:T(2,128)S(1)}, f32[3,40,2,128]{3,2,1,0:T(2,128)S(1)}, u32[]{:S(2)}, u32[]{:S(2)}) collective-permute-start(f32[3,40,2,128]{3,2,1,0:T(2,128)S(1)} %fusion.352), channel_id=1, source_target_pairs={{0,1},{1,2},{2,3},{3,0},{4,5},{5,6},{6,7},{7,4},{8,9},{9,10},{10,1... | collective-permute-start | bytes 368648 | tf_op jit(solution)/shard_map/ppermute | solution.py:277
  120.9 2.9 %fusion.367 = f32[3,12,2,384]{3,1,2,0:T(8,128)S(1)} fusion(f32[]{:T(128)} %bitcast.29, f32[]{:T(128)} %bitcast.28, f32[]{:T(128)} %bitcast.27, s32[384]{0:T(512)} %copy-done.77, s32[384]{0:T(512)} %copy-done.71, s32[384]{0:T(512)} %copy-done.75, s32[384]{0:T(512)} %copy-done.73, pred[384]{0:T(512)(128)(4,1)} %copy-done.84, pred[384]{0:T(512)(128)(4,1)} %copy-done.82, ...), kind=kOutput, calls=%fused_computation.744 | convolution fusion | flops 43106304 | bytes 154380 | tf_op jit(solution)/shard_map/dot_general | solution.py:196
  134.4 5.4 %collective-permute-start.19 = (f32[3,1,2,128]{3,2,1,0:T(2,128)}, f32[3,1,2,128]{3,2,1,0:T(2,128)}, u32[]{:S(2)}, u32[]{:S(2)}) collective-permute-start(f32[3,1,2,128]{3,2,1,0:T(2,128)} %slice.2713), channel_id=1, source_target_pairs={{4,3},{8,7},{12,11},{16,15},{20,19},{24,23},{28,27}} | collective-permute-start | bytes 9224 | tf_op jit(solution)/shard_map/ppermute | solution.py:265
  140.5 2.0 %collective-permute-start.15 = (f32[4,16,640]{2,1,0:T(8,128)}, f32[4,16,640]{2,1,0:T(8,128)}, u32[]{:S(2)}, u32[]{:S(2)}) collective-permute-start(f32[4,16,640]{2,1,0:T(8,128)} %pad_maximum_fusion.57), channel_id=1, source_target_pairs={{0,4},{4,8},{8,12},{12,16},{16,20},{20,24},{24,28},{1,5},{5,9},{9,... | collective-permute-start | bytes 491528 | tf_op jit(solution)/shard_map/ppermute | solution.py:249
  143.3 4.5 %collective-permute-start.16 = (f32[5,16,640]{2,1,0:T(8,128)}, f32[5,16,640]{2,1,0:T(8,128)S(1)}, u32[]{:S(2)}, u32[]{:S(2)}) collective-permute-start(f32[5,16,640]{2,1,0:T(8,128)} %pad_maximum_fusion.53), channel_id=1, source_target_pairs={{4,0},{8,4},{12,8},{16,12},{20,16},{24,20},{28,24},{5,1},{9,5},{13... | collective-permute-start | bytes 614408 | tf_op jit(solution)/shard_map/ppermute | solution.py:254
  149.5 2.8 %fusion = f32[3,4,2,128]{3,2,1,0:T(2,128)S(1)} fusion(f32[3,4,2,384]{3,2,1,0:T(2,128)S(1)} %multiply_reduce_fusion, f32[]{:T(128)} %bitcast.20, f32[]{:T(128)} %bitcast.19, f32[]{:T(128)} %bitcast.18, s32[384]{0:T(512)} %copy-done.77, s32[384]{0:T(512)} %copy-done.71, s32[384]{0:T(512)} %copy-done.75, s32[384]{0:T(512)} %copy-done.73, ...), kind=kOutput, calls=%fused_computation.5 | convolution fusion | flops 14555136 | bytes 68369 | tf_op jit(solution)/shard_map/dot_general | solution.py:207
  152.4 2.1 %collective-permute-start.17 = (f32[3,40,2,128]{3,2,1,0:T(2,128)S(1)}, f32[3,40,2,128]{3,2,1,0:T(2,128)S(1)}, u32[]{:S(2)}, u32[]{:S(2)}) collective-permute-start(f32[3,40,2,128]{3,2,1,0:T(2,128)S(1)} %pad_maximum_fusion.64), channel_id=1, source_target_pairs={{0,1},{1,2},{2,3},{3,0},{4,5},{5,6},{6,7},{7,4},{8,9},{9,10},{10,1... | collective-permute-start | bytes 368648 | tf_op jit(solution)/shard_map/ppermute | solution.py:277
  157.5 2.9 %fusion.365 = f32[3,12,2,384]{3,1,2,0:T(8,128)S(1)} fusion(f32[]{:T(128)} %bitcast.29, f32[]{:T(128)} %bitcast.28, f32[]{:T(128)} %bitcast.27, s32[384]{0:T(512)} %copy-done.77, s32[384]{0:T(512)} %copy-done.71, s32[384]{0:T(512)} %copy-done.75, s32[384]{0:T(512)} %copy-done.73, pred[384]{0:T(512)(128)(4,1)} %copy-done.84, pred[384]{0:T(512)(128)(4,1)} %copy-done.82, ...), kind=kOutput, calls=%fused_computation.743 | convolution fusion | flops 43106304 | bytes 154380 | tf_op jit(solution)/shard_map/dot_general | solution.py:196
  168.4 2.2 %multiply_add_fusion = (f32[6,12,16,384]{3,2,1,0:T(8,128)S(1)}, f32[6,12,16,384]{3,2,1,0:T(8,128)}) fusion(f32[6,12,16,384]{3,2,1,0:T(8,128)S(1)} %fusion.174, f32[6,12,16,384]{3,2,1,0:T(8,128)S(1)} %copy-done.6, f32[6,12,16,384]{3,2,1,0:T(8,128)S(1)} %copy-done.9, f32[12,16,384]{2,1,0:T(8,128)S(1)} %copy-done.29, f32[12,16,384]{2,1,0:T(8,128)S(1)} %copy-done.27, ...), kind=kLoop, calls=%fused_computation | loop fusion | flops 7077888 | bytes 11206656 | tf_op jit(solution)/shard_map/add | solution.py:118
  170.6 2.2 %maximum_maximum_fusion.1 = f32[4,32,128]{2,1,0:T(8,128)} fusion(f32[6,4,32,128]{3,2,1,0:T(8,128)S(1)} %get-tuple-element.30, f32[4,32,128]{2,1,0:T(8,128)S(1)} %copy-done.65, f32[4,32,128]{2,1,0:T(8,128)S(1)} %copy-done.81, f32[4,32,128]{2,1,0:T(8,128)S(1)} %copy-done.4, f32[6,4,32,128]{3,2,1,0:T(8,128)S(1)} %copy-done.32), kind=kLoop, calls=%fused_computation.1314 | loop fusion | flops 8159232 | bytes 1048576 | tf_op jit(solution)/shard_map/max | solution.py:165
  172.8 7.5 %maximum_maximum_fusion = f32[12,16,384]{2,1,0:T(8,128)} fusion(f32[6,12,16,384]{3,2,1,0:T(8,128)S(1)} %get-tuple-element.36, f32[12,16,384]{2,1,0:T(8,128)S(1)} %copy-done.42, f32[12,16,384]{2,1,0:T(8,128)S(1)} %copy-done.80, f32[12,16,384]{2,1,0:T(8,128)S(1)} %copy-done, f32[6,12,16,384]{3,2,1,0:T(8,128)S(1)} %copy-done.3), kind=kLoop, calls=%fused_computation.561 | loop fusion | flops 36716544 | bytes 4718592 | tf_op jit(solution)/shard_map/max | solution.py:165
  (471 shorter events, 95.9 us)
Async XLA Ops:
  0.6 21.0 %copy-start.1 = (f32[6,12,16,384]{3,2,1,0:T(8,128)S(1)}, f32[6,12,16,384]{3,2,1,0:T(8,128)}, u32[]{:S(2)}) copy-start(f32[6,12,16,384]{3,2,1,0:T(8,128)} %param.14) | copy-start | bytes 5308420
  2.9 43.5 %collective-permute-start.4 = (f32[3,1,2,128]{3,2,1,0:T(2,128)}, f32[3,1,2,128]{3,2,1,0:T(2,128)S(1)}, u32[]{:S(2)}, u32[]{:S(2)}) collective-permute-start(f32[3,1,2,128]{3,2,1,0:T(2,128)} %pad_maximum_fusion.127), channel_id=1, source_target_pairs={{4,3},{8,7},{12,11},{16,15},{20,19},{24,23},{28,27}} | collective-permute-start | bytes 9224 | tf_op jit(solution)/shard_map/ppermute | solution.py:265
  11.6 34.1 %collective-permute-start.3 = (f32[3,40,2,128]{3,2,1,0:T(2,128)}, f32[3,40,2,128]{3,2,1,0:T(2,128)}, u32[]{:S(2)}, u32[]{:S(2)}) collective-permute-start(f32[3,40,2,128]{3,2,1,0:T(2,128)} %fusion.354), channel_id=1, source_target_pairs={{1,0},{2,1},{3,2},{0,3},{5,4},{6,5},{7,6},{4,7},{9,8},{10,9},{11,1... | collective-permute-start | bytes 368648 | tf_op jit(solution)/shard_map/ppermute | solution.py:264
  15.5 37.5 %collective-permute-start = (f32[4,16,640]{2,1,0:T(8,128)}, f32[4,16,640]{2,1,0:T(8,128)}, u32[]{:S(2)}, u32[]{:S(2)}) collective-permute-start(f32[4,16,640]{2,1,0:T(8,128)} %pad_maximum_fusion.54), channel_id=1, source_target_pairs={{4,0},{8,4},{12,8},{16,12},{20,16},{24,20},{28,24},{5,1},{9,5},{13... | collective-permute-start | bytes 491528 | tf_op jit(solution)/shard_map/ppermute | solution.py:254
  19.0 36.4 %collective-permute-start.1 = (f32[5,16,640]{2,1,0:T(8,128)}, f32[5,16,640]{2,1,0:T(8,128)}, u32[]{:S(2)}, u32[]{:S(2)}) collective-permute-start(f32[5,16,640]{2,1,0:T(8,128)} %pad_maximum_fusion.50), channel_id=1, source_target_pairs={{0,4},{4,8},{8,12},{12,16},{16,20},{20,24},{24,28},{1,5},{5,9},{9,... | collective-permute-start | bytes 614408 | tf_op jit(solution)/shard_map/ppermute | solution.py:249
  20.9 92.5 %copy-start.69 = (f32[3]{0:T(128)}, f32[3]{0:T(128)S(1)}, u32[]{:S(2)}) copy-start(f32[3]{0:T(128)S(1)} %get-tuple-element.307) | copy-start | bytes 40
  26.8 23.8 %collective-permute-start.2 = (f32[3,40,2,128]{3,2,1,0:T(2,128)}, f32[3,40,2,128]{3,2,1,0:T(2,128)}, u32[]{:S(2)}, u32[]{:S(2)}) collective-permute-start(f32[3,40,2,128]{3,2,1,0:T(2,128)} %fusion.356), channel_id=1, source_target_pairs={{0,1},{1,2},{2,3},{3,0},{4,5},{5,6},{6,7},{7,4},{8,9},{9,10},{10,1... | collective-permute-start | bytes 368648 | tf_op jit(solution)/shard_map/ppermute | solution.py:277
  44.2 76.6 %copy-start.68 = (f32[12]{0:T(128)}, f32[12]{0:T(128)S(1)}, u32[]{:S(2)}) copy-start(f32[12]{0:T(128)S(1)} %mul.2258) | copy-start | bytes 148
  60.5 22.4 %collective-permute-start.9 = (f32[3,1,2,128]{3,2,1,0:T(2,128)S(1)}, f32[3,1,2,128]{3,2,1,0:T(2,128)S(1)}, u32[]{:S(2)}, u32[]{:S(2)}) collective-permute-start(f32[3,1,2,128]{3,2,1,0:T(2,128)S(1)} %slice.2533), channel_id=1, source_target_pairs={{4,3},{8,7},{12,11},{16,15},{20,19},{24,23},{28,27}} | collective-permute-start | bytes 9224 | tf_op jit(solution)/shard_map/ppermute | solution.py:265
  67.1 20.1 %collective-permute-start.5 = (f32[4,16,640]{2,1,0:T(8,128)}, f32[4,16,640]{2,1,0:T(8,128)}, u32[]{:S(2)}, u32[]{:S(2)}) collective-permute-start(f32[4,16,640]{2,1,0:T(8,128)} %pad_maximum_fusion.55), channel_id=1, source_target_pairs={{0,4},{4,8},{8,12},{12,16},{16,20},{20,24},{24,28},{1,5},{5,9},{9,... | collective-permute-start | bytes 491528 | tf_op jit(solution)/shard_map/ppermute | solution.py:249
  69.7 19.9 %collective-permute-start.6 = (f32[5,16,640]{2,1,0:T(8,128)}, f32[5,16,640]{2,1,0:T(8,128)}, u32[]{:S(2)}, u32[]{:S(2)}) collective-permute-start(f32[5,16,640]{2,1,0:T(8,128)} %pad_maximum_fusion.51), channel_id=1, source_target_pairs={{4,0},{8,4},{12,8},{16,12},{20,16},{24,20},{28,24},{5,1},{9,5},{13... | collective-permute-start | bytes 614408 | tf_op jit(solution)/shard_map/ppermute | solution.py:254
  75.0 7.1 %collective-permute-start.8 = (f32[3,40,2,128]{3,2,1,0:T(2,128)}, f32[3,40,2,128]{3,2,1,0:T(2,128)}, u32[]{:S(2)}, u32[]{:S(2)}) collective-permute-start(f32[3,40,2,128]{3,2,1,0:T(2,128)} %pad_maximum_fusion.63), channel_id=1, source_target_pairs={{1,0},{2,1},{3,2},{0,3},{5,4},{6,5},{7,6},{4,7},{9,8},{10,9},{11,1... | collective-permute-start | bytes 368648 | tf_op jit(solution)/shard_map/ppermute | solution.py:264
  80.0 6.9 %collective-permute-start.7 = (f32[3,40,2,128]{3,2,1,0:T(2,128)S(1)}, f32[3,40,2,128]{3,2,1,0:T(2,128)S(1)}, u32[]{:S(2)}, u32[]{:S(2)}) collective-permute-start(f32[3,40,2,128]{3,2,1,0:T(2,128)S(1)} %pad_maximum_fusion.62), channel_id=1, source_target_pairs={{0,1},{1,2},{2,3},{3,0},{4,5},{5,6},{6,7},{7,4},{8,9},{9,10},{10,1... | collective-permute-start | bytes 368648 | tf_op jit(solution)/shard_map/ppermute | solution.py:277
  99.5 19.8 %collective-permute-start.14 = (f32[3,1,2,128]{3,2,1,0:T(2,128)}, f32[3,1,2,128]{3,2,1,0:T(2,128)}, u32[]{:S(2)}, u32[]{:S(2)}) collective-permute-start(f32[3,1,2,128]{3,2,1,0:T(2,128)} %pad_maximum_fusion.126), channel_id=1, source_target_pairs={{4,3},{8,7},{12,11},{16,15},{20,19},{24,23},{28,27}} | collective-permute-start | bytes 9224 | tf_op jit(solution)/shard_map/ppermute | solution.py:265
  103.7 14.8 %collective-permute-start.13 = (f32[3,40,2,128]{3,2,1,0:T(2,128)}, f32[3,40,2,128]{3,2,1,0:T(2,128)}, u32[]{:S(2)}, u32[]{:S(2)}) collective-permute-start(f32[3,40,2,128]{3,2,1,0:T(2,128)} %fusion.350), channel_id=1, source_target_pairs={{1,0},{2,1},{3,2},{0,3},{5,4},{6,5},{7,6},{4,7},{9,8},{10,9},{11,1... | collective-permute-start | bytes 368648 | tf_op jit(solution)/shard_map/ppermute | solution.py:264
  104.4 20.7 %collective-permute-start.10 = (f32[4,16,640]{2,1,0:T(8,128)}, f32[4,16,640]{2,1,0:T(8,128)}, u32[]{:S(2)}, u32[]{:S(2)}) collective-permute-start(f32[4,16,640]{2,1,0:T(8,128)} %pad_maximum_fusion.56), channel_id=1, source_target_pairs={{4,0},{8,4},{12,8},{16,12},{20,16},{24,20},{28,24},{5,1},{9,5},{13... | collective-permute-start | bytes 491528 | tf_op jit(solution)/shard_map/ppermute | solution.py:254
  107.0 20.5 %collective-permute-start.11 = (f32[5,16,640]{2,1,0:T(8,128)}, f32[5,16,640]{2,1,0:T(8,128)}, u32[]{:S(2)}, u32[]{:S(2)}) collective-permute-start(f32[5,16,640]{2,1,0:T(8,128)} %pad_maximum_fusion.52), channel_id=1, source_target_pairs={{0,4},{4,8},{8,12},{12,16},{16,20},{20,24},{24,28},{1,5},{5,9},{9,... | collective-permute-start | bytes 614408 | tf_op jit(solution)/shard_map/ppermute | solution.py:249
  116.5 8.4 %collective-permute-start.12 = (f32[3,40,2,128]{3,2,1,0:T(2,128)S(1)}, f32[3,40,2,128]{3,2,1,0:T(2,128)S(1)}, u32[]{:S(2)}, u32[]{:S(2)}) collective-permute-start(f32[3,40,2,128]{3,2,1,0:T(2,128)S(1)} %fusion.352), channel_id=1, source_target_pairs={{0,1},{1,2},{2,3},{3,0},{4,5},{5,6},{6,7},{7,4},{8,9},{9,10},{10,1... | collective-permute-start | bytes 368648 | tf_op jit(solution)/shard_map/ppermute | solution.py:277
  128.8 25.6 %copy-start.40 = (f32[3,4,32,128]{3,2,1,0:T(8,128)}, f32[3,4,32,128]{3,2,1,0:T(8,128)S(1)}, u32[]{:S(2)}) copy-start(f32[3,4,32,128]{3,2,1,0:T(8,128)S(1)} %fusion.348) | copy-start | bytes 589828
  134.4 20.8 %collective-permute-start.19 = (f32[3,1,2,128]{3,2,1,0:T(2,128)}, f32[3,1,2,128]{3,2,1,0:T(2,128)}, u32[]{:S(2)}, u32[]{:S(2)}) collective-permute-start(f32[3,1,2,128]{3,2,1,0:T(2,128)} %slice.2713), channel_id=1, source_target_pairs={{4,3},{8,7},{12,11},{16,15},{20,19},{24,23},{28,27}} | collective-permute-start | bytes 9224 | tf_op jit(solution)/shard_map/ppermute | solution.py:265
  140.5 21.1 %collective-permute-start.15 = (f32[4,16,640]{2,1,0:T(8,128)}, f32[4,16,640]{2,1,0:T(8,128)}, u32[]{:S(2)}, u32[]{:S(2)}) collective-permute-start(f32[4,16,640]{2,1,0:T(8,128)} %pad_maximum_fusion.57), channel_id=1, source_target_pairs={{0,4},{4,8},{8,12},{12,16},{16,20},{20,24},{24,28},{1,5},{5,9},{9,... | collective-permute-start | bytes 491528 | tf_op jit(solution)/shard_map/ppermute | solution.py:249
  143.3 20.8 %collective-permute-start.16 = (f32[5,16,640]{2,1,0:T(8,128)}, f32[5,16,640]{2,1,0:T(8,128)S(1)}, u32[]{:S(2)}, u32[]{:S(2)}) collective-permute-start(f32[5,16,640]{2,1,0:T(8,128)} %pad_maximum_fusion.53), channel_id=1, source_target_pairs={{4,0},{8,4},{12,8},{16,12},{20,16},{24,20},{28,24},{5,1},{9,5},{13... | collective-permute-start | bytes 614408 | tf_op jit(solution)/shard_map/ppermute | solution.py:254
  148.5 5.9 %collective-permute-start.18 = (f32[3,40,2,128]{3,2,1,0:T(2,128)}, f32[3,40,2,128]{3,2,1,0:T(2,128)}, u32[]{:S(2)}, u32[]{:S(2)}) collective-permute-start(f32[3,40,2,128]{3,2,1,0:T(2,128)} %pad_maximum_fusion.65), channel_id=1, source_target_pairs={{1,0},{2,1},{3,2},{0,3},{5,4},{6,5},{7,6},{4,7},{9,8},{10,9},{11,1... | collective-permute-start | bytes 368648 | tf_op jit(solution)/shard_map/ppermute | solution.py:264
  152.4 9.0 %collective-permute-start.17 = (f32[3,40,2,128]{3,2,1,0:T(2,128)S(1)}, f32[3,40,2,128]{3,2,1,0:T(2,128)S(1)}, u32[]{:S(2)}, u32[]{:S(2)}) collective-permute-start(f32[3,40,2,128]{3,2,1,0:T(2,128)S(1)} %pad_maximum_fusion.64), channel_id=1, source_target_pairs={{0,1},{1,2},{2,3},{3,0},{4,5},{5,6},{6,7},{7,4},{8,9},{9,10},{10,1... | collective-permute-start | bytes 368648 | tf_op jit(solution)/shard_map/ppermute | solution.py:277
  (81 other events, 351.2 us)
where the time goes:
time: 184 us; the launch traced here: 180 us
  other arithmetic  51 us (28%)
  starting transfers between devices  50.9 us (28%)
  local copies, waits for them, and re-layouts  47.5 us (26%)
  matrix products  22.1 us (12%)
  Pallas kernels  4.45 us (2%)
  between operations  4.25 us (2%)
    ppermute x4, starting transfers between devices, exchange(): lax.ppermute(coarse_head[:, :1], ('lat', 'depth'), [((i + 1) * depths, i...  20.6 us
    ppermute x4, starting transfers between devices, exchange(): lax.ppermute(lateral_message(high_rows(fine), high_rows(coarse)), 'lat',...  13.7 us
    dot_general x4, matrix products, interpolate(): spread = jnp.dot(flat, y_spread, precision=lax.Precision.HIGHEST)  11.6 us
    slice x16, local copies, waits for them, and re-layouts, cut_rows(): parts.append(block[begin:begin + kind[side]])  11.3 us
    dot_general x4, matrix products, restrict(): gathered = jnp.dot(flat, y_gather, precision=lax.Precision.HIGHEST)  10.5 us
    max x2, other arithmetic, strain_peak(): return jnp.maximum(peak, principal)  9.71 us
    ppermute x4, starting transfers between devices, exchange(): lax.ppermute(lateral_message(low_rows(fine), low_rows(coarse)), 'lat', [(...  8.7 us
    ppermute x4, starting transfers between devices, exchange(): lax.ppermute(tail, 'depth', [(i, (i + 1) % depths) for i in range(depths)])  7.86 us
  transfers between devices with their start and end apart: 20, of which 0 were waited for; matrix products, arithmetic and copies ran while one was open for 45% of the time, Pallas kernels for 2%

commit v1 on v0

v1 whole, which is shorter than its diff:
```python
import functools

import jax
import jax.numpy as jnp
from jax import lax
from jax.experimental import pallas as pl
from jax.experimental.pallas import tpu as pltpu
from jax.sharding import PartitionSpec as P

STEPS = 2
LANES = 128
ROWS = 8

TIME_STEP = 0.4
NEAR = 9.0 / 8.0
FAR = 1.0 / 27.0
TINY = 1e-18

FORWARD = (1, 2)
BACKWARD = (2, 1)
STRESS_X = ((0, FORWARD), (3, BACKWARD), (4, BACKWARD))
STRESS_Z = ((4, BACKWARD), (5, BACKWARD), (2, FORWARD))
VELOCITY_X = ((0, BACKWARD), (1, FORWARD), (2, FORWARD))
VELOCITY_Z = ((0, FORWARD), (1, FORWARD), (2, BACKWARD))

BUOYANCY, LAME, SHEAR, DECAY, DAMPING, VOLUMETRIC, SCALE = range(7)

MESH = pl.DeviceIdType.MESH
EXACT = lax.Precision.HIGHEST


def zone_columns(table_ref):
    lane = lax.broadcasted_iota(jnp.int32, (ROWS, LANES), 1)
    columns = []
    for column in range(table_ref.shape[1]):
        value = jnp.full((ROWS, LANES), table_ref[0, column], jnp.float32)
        for level in range(1, table_ref.shape[0]):
            value = jnp.where(lane == level, table_ref[level, column], value)
        columns.append(value)
    return columns


def strain_tables(columns):
    lame, shear = columns[1], columns[2]
    return [lame / (3.0 * lame + 2.0 * shear), 0.5 / shear]


def step_tables(columns, spacing):
    buoyancy, lame, shear, decay, damping = columns
    return [
        buoyancy * (TIME_STEP * NEAR / spacing),
        lame * (NEAR / spacing),
        shear * (2.0 * NEAR / spacing),
        decay,
        damping * (1.0 - decay),
    ]


def lookup(table, zone):
    parts = [
        jnp.take_along_axis(
            table, zone[begin : begin + ROWS], axis=1, mode="promise_in_bounds"
        )
        for begin in range(0, zone.shape[0], ROWS)
    ]
    return jnp.concatenate(parts, axis=0)


def rotation(low, high, pivot):
    half = 0.5 * (high - low)
    size = jnp.maximum(jnp.abs(half), TINY)
    square = size * size + pivot * pivot
    radius = square * lax.rsqrt(square)
    reach = size + radius
    weight = lax.rsqrt((radius + radius) * reach)
    sign = jnp.where(half >= 0, 1.0, -1.0)
    middle = low + half
    offset = sign * radius
    return reach * weight, sign * (pivot * weight), middle - offset, middle + offset


def largest(low, high, pivot):
    half = 0.5 * (high - low)
    size = jnp.maximum(jnp.abs(half), TINY)
    square = size * size + pivot * pivot
    return low + half + square * lax.rsqrt(square)


def principal(stress, volumetric, scale):
    a00, a11, a22, a01, a02, a12 = stress
    shift = volumetric * (a00 + a11 + a22)
    cosine, sine, a00, a11 = rotation(a00, a11, a01)
    a02, a12 = cosine * a02 - sine * a12, sine * a02 + cosine * a12
    for sweep in range(3):
        if sweep > 0:
            cosine, sine, a00, a11 = rotation(a00, a11, a01)
            a02, a12 = cosine * a02, sine * a02
        cosine, sine, a00, a22 = rotation(a00, a22, a02)
        a01, a12 = -(sine * a12), cosine * a12
        if sweep < 2:
            cosine, sine, a11, a22 = rotation(a11, a22, a12)
            a01, a02 = cosine * a01, sine * a01
    return (jnp.maximum(a00, largest(a11, a22, a12)) - shift) * scale


def shifted_y(tiles, offset):
    lane = lax.broadcasted_iota(jnp.int32, tiles[0].shape, 1)
    rolled = [pltpu.roll(tile, (-offset) % LANES, 1) for tile in tiles]
    zero = jnp.zeros_like(tiles[0])
    if offset > 0:
        outside, beside = lane >= LANES - offset, rolled[1:] + [zero]
    else:
        outside, beside = lane < -offset, [zero] + rolled[:-1]
    return [jnp.where(outside, other, own) for other, own in zip(beside, rolled)]


def difference_y(tiles, kind):
    if kind == FORWARD:
        near = [a - b for a, b in zip(shifted_y(tiles, 1), tiles)]
        far = [a - b for a, b in zip(shifted_y(tiles, 2), shifted_y(tiles, -1))]
    else:
        near = [a - b for a, b in zip(tiles, shifted_y(tiles, -1))]
        far = [a - b for a, b in zip(shifted_y(tiles, 1), shifted_y(tiles, -2))]
    return list(zip(near, far))


def difference(at, kind):
    if kind == FORWARD:
        return at(1) - at(0), at(2) - at(-1)
    return at(0) - at(-1), at(1) - at(-2)


def total(*pairs):
    near = sum(pair[0] for pair in pairs[1:]) + pairs[0][0]
    far = sum(pair[1] for pair in pairs[1:]) + pairs[0][1]
    return near - FAR * far


class Field:
    def __init__(self, spacing, refs):
        self.spacing = spacing
        (
            self.stress,
            self.velocity,
            self.memory,
            self.peak,
            self.zone,
            self.props,
            self.below_x,
            self.above_x,
            self.around_z,
        ) = refs
        self.tiles, self.rows, self.depth, _ = self.peak.shape

    def cells(self, ref, part, tile, row, dx=0, dz=0):
        return ref[part, tile, row + (2 + dx), pl.ds(ROWS + dz, self.depth), :]

    def along_x(self, ref, part, tile, row, kind):
        return difference(lambda d: self.cells(ref, part, tile, row, dx=d), kind)

    def along_z(self, ref, part, tile, row, kind):
        return difference(lambda d: self.cells(ref, part, tile, row, dz=d), kind)

    def along_y(self, ref, part, row, kind):
        tiles = [self.cells(ref, part, tile, row) for tile in range(self.tiles)]
        return difference_y(tiles, kind)

    def each_row(self, body, begin=0, end=None):
        def step(row, carry):
            body(row)
            return carry

        lax.fori_loop(begin, self.rows if end is None else end, step, 0)

    def clear(self):
        stress, velocity, depth = self.stress, self.velocity, self.depth
        tile_zero = jnp.zeros((ROWS, LANES), jnp.float32)
        zero = jnp.zeros((depth, LANES), jnp.float32)

        def body(row):
            for tile in range(self.tiles):
                for ref, parts in ((stress, (2, 4, 5)), (velocity, (0, 1, 2))):
                    for part in parts:
                        ref[part, tile, row + 2, 0:ROWS, :] = tile_zero
                        ref[part, tile, row + 2, pl.ds(ROWS + depth, ROWS), :] = tile_zero
                for turn in range(2 * STEPS):
                    for slot in range(3):
                        self.around_z[turn, slot, tile, row, pl.ds(ROWS, ROWS), :] = tile_zero

        self.each_row(body)
        for tile in range(self.tiles):
            for ref, parts in ((stress, (0, 3, 4)), (velocity, (0, 1, 2))):
                for part in parts:
                    for row in (0, 1, self.rows + 2, self.rows + 3):
                        ref[part, tile, row, pl.ds(ROWS, depth), :] = zero

    def clear_x(self, side):
        ref = self.below_x if side == 0 else self.above_x
        zero = jnp.zeros((self.depth, LANES), jnp.float32)

        def body(turn, carry):
            for slot in range(3):
                for tile in range(self.tiles):
                    for row in range(2):
                        ref[turn, slot, tile, row] = zero
            return carry

        lax.fori_loop(0, 2 * STEPS, body, 0)

    def clear_z(self, side):
        zero = jnp.zeros((ROWS, LANES), jnp.float32)

        def body(row):
            for turn in range(2 * STEPS):
                for slot in range(3):
                    for tile in range(self.tiles):
                        self.around_z[turn, slot, tile, row, pl.ds(2 * ROWS * side, ROWS), :] = zero

        self.each_row(body)

    def fill_props(self, columns):
        tables = step_tables(columns, self.spacing) + strain_tables(columns)

        def body(row):
            for tile in range(self.tiles):
                zone = self.zone[tile, row]
                for index, table in enumerate(tables):
                    self.props[index, tile, row] = lookup(table, zone)

        self.each_row(body)

    def velocity_inner(self, row):
        stress, velocity = self.stress, self.velocity
        across = [
            self.along_y(stress, 3, row, BACKWARD),
            self.along_y(stress, 1, row, FORWARD),
            self.along_y(stress, 5, row, BACKWARD),
        ]
        for part in range(3):
            for tile in range(self.tiles):
                (field_x, kind_x), (field_z, kind_z) = STRESS_X[part], STRESS_Z[part]
                accel = total(
                    self.along_x(stress, field_x, tile, row, kind_x),
                    across[part][tile],
                    self.along_z(stress, field_z, tile, row, kind_z),
                )
                old = self.cells(velocity, part, tile, row)
                buoyancy = self.props[BUOYANCY, tile, row]
                velocity[part, tile, row + 2, pl.ds(ROWS, self.depth), :] = old + buoyancy * accel

    def outer_rows(self, turn, slot, tile, kind):
        below, above = self.below_x.at[turn, slot, tile], self.above_x.at[turn, slot, tile]
        last = self.rows - 1
        if kind == FORWARD:
            return [
                (0, FAR * below[1]),
                (last, above[0] - FAR * above[1]),
                (last - 1, -FAR * above[0]),
            ]
        return [
            (0, FAR * below[0] - below[1]),
            (1, FAR * below[1]),
            (last, -FAR * above[0]),
        ]

    def outer_layers(self, turn, slot, tile, row, kind):
        at = self.around_z.at[turn, slot, tile, row]

        def lower(distance):
            return at[pl.ds(ROWS - distance, ROWS), :]

        def upper(distance):
            return at[pl.ds(ROWS + distance, ROWS), :]

        if kind == FORWARD:
            return FAR * lower(1), upper(1) - FAR * upper(2)
        return FAR * lower(2) - lower(1), -FAR * upper(1)

    def ends(self):
        return (0, self.depth - ROWS)

    def velocity_outer(self, turn):
        velocity, depth = self.velocity, self.depth
        for part in range(3):
            for tile in range(self.tiles):
                for row, term in self.outer_rows(turn, part, tile, STRESS_X[part][1]):
                    place = velocity.at[part, tile, row + 2, pl.ds(ROWS, depth), :]
                    place[...] = place[...] + self.props[BUOYANCY, tile, row] * term

        def body(row):
            for part in range(3):
                for tile in range(self.tiles):
                    terms = self.outer_layers(turn, part, tile, row, STRESS_Z[part][1])
                    for begin, term in zip(self.ends(), terms):
                        place = velocity.at[part, tile, row + 2, pl.ds(ROWS + begin, ROWS), :]
                        buoyancy = self.props[BUOYANCY, tile, row, pl.ds(begin, ROWS), :]
                        place[...] = place[...] + buoyancy * term

        self.each_row(body)

    def stress_inner(self, row):
        velocity, stress, memory = self.velocity, self.stress, self.memory
        across_y = self.along_y(velocity, 1, row, BACKWARD)
        across_x = self.along_y(velocity, 0, row, FORWARD)
        across_z = self.along_y(velocity, 2, row, FORWARD)
        for tile in range(self.tiles):
            lame, shear, decay, damping = (
                self.props[index, tile, row] for index in (LAME, SHEAR, DECAY, DAMPING)
            )
            normal_x = total(self.along_x(velocity, 0, tile, row, BACKWARD))
            normal_y = total(across_y[tile])
            normal_z = total(self.along_z(velocity, 2, tile, row, BACKWARD))
            shear_xy = total(across_x[tile], self.along_x(velocity, 1, tile, row, FORWARD))
            shear_xz = total(
                self.along_z(velocity, 0, tile, row, FORWARD),
                self.along_x(velocity, 2, tile, row, FORWARD),
            )
            shear_yz = total(across_z[tile], self.along_z(velocity, 1, tile, row, FORWARD))
            volume = lame * (normal_x + normal_y + normal_z)
            half = 0.5 * shear
            rates = [
                volume + shear * normal_x,
                volume + shear * normal_y,
                volume + shear * normal_z,
                half * shear_xy,
                half * shear_xz,
                half * shear_yz,
            ]
            kept = 0.5 * TIME_STEP * (1.0 + decay)
            gained = TIME_STEP - 0.5 * TIME_STEP * damping
            for part, rate in enumerate(rates):
                past = memory[part, tile, row]
                memory[part, tile, row] = decay * past - damping * rate
                old = self.cells(stress, part, tile, row)
                stress[part, tile, row + 2, pl.ds(ROWS, self.depth), :] = (
                    old + kept * past + gained * rate
                )

    def add_rates(self, rates, tile, row, begin, count):
        damping = self.props[DAMPING, tile, row, pl.ds(begin, count), :]
        gained = TIME_STEP - 0.5 * TIME_STEP * damping
        for part, rate in rates:
            place = self.memory.at[part, tile, row, pl.ds(begin, count), :]
            place[...] = place[...] - damping * rate
            place = self.stress.at[part, tile, row + 2, pl.ds(ROWS + begin, count), :]
            place[...] = place[...] + gained * rate

    def normal_rates(self, term, along, tile, row, begin, count):
        lame = self.props[LAME, tile, row, pl.ds(begin, count), :]
        shear = self.props[SHEAR, tile, row, pl.ds(begin, count), :]
        volume = lame * term
        return [(part, volume + shear * term if part == along else volume) for part in range(3)]

    def shear_rates(self, term, part, tile, row, begin, count):
        shear = self.props[SHEAR, tile, row, pl.ds(begin, count), :]
        return [(part, (0.5 * shear) * term)]

    def stress_outer(self, turn):
        depth = self.depth
        for tile in range(self.tiles):
            for row, term in self.outer_rows(turn, 0, tile, BACKWARD):
                rates = self.normal_rates(term, 0, tile, row, 0, depth)
                self.add_rates(rates, tile, row, 0, depth)
            for slot, part in ((1, 3), (2, 4)):
                for row, term in self.outer_rows(turn, slot, tile, FORWARD):
                    rates = self.shear_rates(term, part, tile, row, 0, depth)
                    self.add_rates(rates, tile, row, 0, depth)

        def body(row):
            for tile in range(self.tiles):
                normal = self.outer_layers(turn, 2, tile, row, BACKWARD)
                shear_xz = self.outer_layers(turn, 0, tile, row, FORWARD)
                shear_yz = self.outer_layers(turn, 1, tile, row, FORWARD)
                for end, begin in enumerate(self.ends()):
                    rates = (
                        self.normal_rates(normal[end], 2, tile, row, begin, ROWS)
                        + self.shear_rates(shear_xz[end], 4, tile, row, begin, ROWS)
                        + self.shear_rates(shear_yz[end], 5, tile, row, begin, ROWS)
                    )
                    self.add_rates(rates, tile, row, begin, ROWS)

        self.each_row(body)

    def raise_peak(self, row):
        for tile in range(self.tiles):
            strain = principal(
                [self.cells(self.stress, part, tile, row) for part in range(6)],
                self.props[VOLUMETRIC, tile, row],
                self.props[SCALE, tile, row],
            )
            self.peak[tile, row] = jnp.maximum(self.peak[tile, row], strain)


def spread_matrix(interp_ref, coarse_cells, fine_cells):
    coarse = lax.broadcasted_iota(jnp.int32, (coarse_cells, fine_cells), 0)
    fine = lax.broadcasted_iota(jnp.int32, (coarse_cells, fine_cells), 1)
    matrix = jnp.zeros((coarse_cells, fine_cells), jnp.float32)
    for phase in range(3):
        share = interp_ref[1, phase].astype(jnp.float32) / 8.0
        matrix = jnp.where(fine == 3 * coarse + phase, share, matrix)
        matrix = jnp.where(fine == 3 * coarse - 3 + phase, 1.0 - share, matrix)
    return matrix


def gather_matrix(restrict_ref, coarse_cells, fine_cells):
    fine = lax.broadcasted_iota(jnp.int32, (fine_cells, coarse_cells), 0)
    coarse = lax.broadcasted_iota(jnp.int32, (fine_cells, coarse_cells), 1)
    matrix = jnp.zeros((fine_cells, coarse_cells), jnp.float32)
    for phase in range(3):
        weight = restrict_ref[1, phase].astype(jnp.float32)
        matrix = jnp.where(fine == 3 * coarse + phase, weight, matrix)
    return matrix


def lift_matrix(interp_ref, fine_rows, rows):
    target = lax.broadcasted_iota(jnp.int32, (2 * fine_rows, 2 * rows), 0)
    source = lax.broadcasted_iota(jnp.int32, (2 * fine_rows, 2 * rows), 1)
    matrix = jnp.zeros((2 * fine_rows, 2 * rows), jnp.float32)
    for phase in range(3):
        share = interp_ref[0, phase].astype(jnp.float32) / 8.0
        for ghost in range(2):
            for layer in range(2):
                blend = (2.0 if ghost == layer else 1.0) / 3.0
                for ahead in range(2):
                    weight = (share if ahead == 0 else 1.0 - share) * blend
                    base = 6 * (source - layer * rows - ahead) + 2 * phase + ghost
                    inside = (source >= layer * rows + ahead) & (source < (layer + 1) * rows)
                    matrix = jnp.where((target == base) & inside, weight, matrix)
    return matrix


class Coupling:
    def __init__(self, fine, coarse, interp_ref, restrict_ref, refs):
        self.fine, self.coarse = fine, coarse
        self.interp_ref, self.restrict_ref = interp_ref, restrict_ref
        self.heads, self.lifted, self.layers, self.spread, self.gather = refs
        self.block = self.heads.shape[2] // 2

    def clear(self):
        coarse_cells, fine_cells = self.spread.shape
        self.spread[...] = spread_matrix(self.interp_ref, coarse_cells, fine_cells)
        self.gather[...] = gather_matrix(self.restrict_ref, coarse_cells, fine_cells)

    def restrict(self, turn, ref, along_z):
        fine, coarse = self.fine, self.coarse
        weight = [self.restrict_ref[0, phase].astype(jnp.float32) for phase in range(3)]
        weight_y = [self.restrict_ref[1, phase].astype(jnp.float32) for phase in range(3)]
        mass = 3.0 * (weight[0] + weight[1] + weight[2]) * (weight_y[0] + weight_y[1] + weight_y[2])
        for slot, (part, _) in enumerate(along_z):
            for row in range(coarse.rows):
                begin = (slot * coarse.rows + row) * ROWS
                for tile in range(fine.tiles):
                    block = sum(
                        weight[phase]
                        * ref[part, tile, 2 + 3 * row + phase, pl.ds(fine.depth, ROWS), :]
                        for phase in range(3)
                    )
                    self.layers[begin : begin + ROWS, tile * LANES : (tile + 1) * LANES] = block
        gathered = jnp.dot(
            self.layers[...], self.gather[...], precision=EXACT, preferred_element_type=jnp.float32
        )
        gathered = gathered / jnp.full(gathered.shape, mass, jnp.float32)
        for slot in range(3):
            for row in range(coarse.rows):
                begin = (slot * coarse.rows + row) * ROWS
                for tile in range(coarse.tiles):
                    block = gathered[begin : begin + ROWS, tile * LANES : (tile + 1) * LANES]
                    block = block + pltpu.roll(block, 1, 0) + pltpu.roll(block, 2, 0)
                    self.lifted[turn, slot, tile, row, 6:7, :] = block[4:5]
                    self.lifted[turn, slot, tile, row, 7:8, :] = block[7:8]

    def interpolate(self, turn):
        fine = self.fine
        lift = lift_matrix(self.interp_ref, fine.rows, self.block)
        lifted = [
            jnp.dot(lift, self.heads[turn, slot], precision=EXACT, preferred_element_type=jnp.float32)
            for slot in range(3)
        ]
        ghosts = jnp.dot(
            jnp.concatenate(lifted, axis=0),
            self.spread[...],
            precision=EXACT,
            preferred_element_type=jnp.float32,
        )
        for slot in range(3):
            for row in range(fine.rows):
                begin = 2 * (slot * fine.rows + row)
                for tile in range(fine.tiles):
                    fine.around_z[turn, slot, tile, row, 2 * ROWS : 2 * ROWS + 2, :] = ghosts[
                        begin : begin + 2, tile * LANES : (tile + 1) * LANES
                    ]


class Place:
    def __init__(self):
        self.lat, self.depth = lax.axis_index("lat"), lax.axis_index("depth")
        self.lats, self.depths = lax.axis_size("lat"), lax.axis_size("depth")
        lat, depth = self.lat, self.depth
        has_next, has_previous = lat < self.lats - 1, lat > 0
        has_lower, has_upper = depth < self.depths - 1, depth > 0
        top, bottom = depth == 0, depth == self.depths - 1
        self.routes = {
            "head": (lat, self.depths - 1, top, bottom),
            "corner": (lat - 1, self.depths - 1, top & has_previous, bottom & has_next),
            "lift": (lat, 0, bottom, top),
            "next": (lat + 1, depth, has_next, has_previous),
            "previous": (lat - 1, depth, has_previous, has_next),
            "down": (lat, depth + 1, has_lower, has_upper),
            "up": (lat, depth - 1, has_upper, has_lower),
        }
        self.top, self.bottom = top, bottom

    def target(self, route):
        lat, depth = self.routes[route][:2]
        return {"lat": lat, "depth": depth}

    def greet(self):
        barrier = pltpu.get_barrier_semaphore()
        lat, depth = self.lat, self.depth
        peers = [
            (lat + 1, depth, lat < self.lats - 1),
            (lat - 1, depth, lat > 0),
            (lat, depth + 1, depth < self.depths - 1),
            (lat, depth - 1, depth > 0),
            (lat, self.depths - 1, self.top),
            (lat, 0, self.bottom),
            (lat - 1, self.depths - 1, self.top & (lat > 0)),
            (lat + 1, 0, self.bottom & (lat < self.lats - 1)),
        ]
        for peer_lat, peer_depth, present in peers:

            @pl.when(present)
            def _():
                pl.semaphore_signal(
                    barrier,
                    inc=1,
                    device_id={"lat": peer_lat, "depth": peer_depth},
                    device_id_type=MESH,
                )

        return barrier, sum(present.astype(jnp.int32) for _, _, present in peers)


class Exchange:
    def __init__(self, turn, place, fine, coarse, coupling, velocity, sems):
        self.place = place
        along_x = VELOCITY_X if velocity else STRESS_X
        along_z = VELOCITY_Z if velocity else STRESS_Z
        self.messages = {route: [] for route in place.routes}
        self.send_sems, self.recv_sems, self.count, self.turn = sems[0], sems[1], 0, turn
        ref = coarse.velocity if velocity else coarse.stress
        block = coupling.block
        for slot, (part, (low, _)) in enumerate(along_z):
            for layer in range(2):
                for tile in range(coarse.tiles):
                    source = ref.at[part, tile, :, ROWS + layer, :]
                    lanes = pl.ds(tile * LANES, LANES)
                    begin = layer * block
                    self.add(
                        "head",
                        source.at[pl.ds(2, coarse.rows), :],
                        coupling.heads.at[turn, slot, pl.ds(begin, coarse.rows), lanes],
                    )
                    self.add(
                        "corner",
                        source.at[pl.ds(2, 1), :],
                        coupling.heads.at[turn, slot, pl.ds(begin + coarse.rows, 1), lanes],
                    )
            self.add(
                "lift",
                coupling.lifted.at[turn, slot, :, :, pl.ds(ROWS - low, low), :],
                coarse.around_z.at[turn, slot, :, :, pl.ds(ROWS - low, low), :],
            )
        for grid in (fine, coarse):
            ref = grid.velocity if velocity else grid.stress
            inner = pl.ds(ROWS, grid.depth)
            for slot, (part, (low, high)) in enumerate(along_x):
                self.add(
                    "next",
                    ref.at[part, :, pl.ds(2 + grid.rows - low, low), inner, :],
                    grid.below_x.at[turn, slot, :, pl.ds(2 - low, low), :, :],
                )
                self.add(
                    "previous",
                    ref.at[part, :, pl.ds(2, high), inner, :],
                    grid.above_x.at[turn, slot, :, pl.ds(0, high), :, :],
                )
            for slot, (part, (low, high)) in enumerate(along_z):
                rows = pl.ds(2, grid.rows)
                self.add(
                    "down",
                    ref.at[part, :, rows, pl.ds(ROWS + grid.depth - low, low), :],
                    grid.around_z.at[turn, slot, :, :, pl.ds(ROWS - low, low), :],
                )
                self.add(
                    "up",
                    ref.at[part, :, rows, pl.ds(ROWS, high), :],
                    grid.around_z.at[turn, slot, :, :, pl.ds(2 * ROWS, high), :],
                )

    def add(self, route, source, target):
        copy = pltpu.make_async_remote_copy(
            src_ref=source,
            dst_ref=target,
            send_sem=self.send_sems.at[self.turn, self.count],
            recv_sem=self.recv_sems.at[self.turn, self.count],
            device_id=self.place.target(route),
            device_id_type=MESH,
        )
        self.messages[route].append(copy)
        self.count += 1

    def send(self, *routes):
        for route in routes or self.messages:

            @pl.when(self.place.routes[route][2])
            def _():
                for copy in self.messages[route]:
                    copy.start()

    def receive(self, *routes):
        for route in routes or self.messages:

            @pl.when(self.place.routes[route][3])
            def _():
                for copy in self.messages[route]:
                    copy.wait_recv()

    def sent(self):
        for route in self.messages:

            @pl.when(self.place.routes[route][2])
            def _():
                for copy in self.messages[route]:
                    copy.wait_send()


MESSAGES = 64


def waves_kernel(counts, *refs):
    refs = list(refs)

    def take(count):
        taken = refs[:count]
        del refs[:count]
        return taken

    table_ref, interp_ref, restrict_ref = take(3)
    inputs = [take(5), take(5)]
    outputs = [take(4), take(4)]
    fine, coarse = Field(1.0, take(9)), Field(3.0, take(9))
    coupling = Coupling(fine, coarse, interp_ref, restrict_ref, take(5))
    load_sems, store_sems, send_sems, recv_sems = take(4)
    place = Place()
    grids = (fine, coarse)

    loads, stores = {}, {}
    for grid, (velocity, stress, memory, peak, zone) in zip(grids, inputs):
        inner_rows, inner = pl.ds(2, grid.rows), pl.ds(ROWS, grid.depth)
        pairs = [
            ("zone", zone, grid.zone, None),
            ("stress", stress, grid.stress, inner),
            ("velocity", velocity, grid.velocity, inner),
            ("memory", memory, grid.memory, None),
            ("peak", peak, grid.peak, None),
        ]
        for name, source, target, padded in pairs:
            for tile in range(grid.tiles):
                lanes = pl.ds(tile * LANES, LANES)
                if name in ("zone", "peak"):
                    source_part, target_part = source.at[:, :, lanes], target.at[tile]
                elif padded is None:
                    source_part, target_part = source.at[:, :, :, lanes], target.at[:, tile]
                else:
                    source_part = source.at[:, :, :, lanes]
                    target_part = target.at[:, tile, inner_rows, padded, :]
                index = sum(len(group) for group in loads.values())
                copy = pltpu.make_async_copy(source_part, target_part, load_sems.at[index])
                loads.setdefault(name, []).append(copy)
    for grid, (velocity, stress, memory, peak) in zip(grids, outputs):
        inner_rows, inner = pl.ds(2, grid.rows), pl.ds(ROWS, grid.depth)
        for tile in range(grid.tiles):
            lanes = pl.ds(tile * LANES, LANES)
            for name, source_part, target_part in (
                ("velocity", grid.velocity.at[:, tile, inner_rows, inner, :], velocity.at[:, :, :, lanes]),
                ("stress", grid.stress.at[:, tile, inner_rows, inner, :], stress.at[:, :, :, lanes]),
                ("memory", grid.memory.at[:, tile], memory.at[:, :, :, lanes]),
                ("peak", grid.peak.at[tile], peak.at[:, :, lanes]),
            ):
                index = sum(len(group) for group in stores.values())
                copy = pltpu.make_async_copy(source_part, target_part, store_sems.at[index])
                stores.setdefault(name, []).append(copy)

    def start(group):
        for copy in group:
            copy.start()

    def finish(group):
        for copy in group:
            copy.wait()

    for name in ("zone", "stress", "velocity", "memory", "peak"):
        start(loads[name])
    coupling.heads[...] = jnp.zeros(coupling.heads.shape, jnp.float32)
    barrier, peers = place.greet()

    for grid in grids:
        grid.clear()

    @pl.when(place.top)
    def _():
        fine.clear_z(0)

    @pl.when(place.bottom)
    def _():
        coarse.clear_z(1)

    for side, outside in ((0, place.lat == 0), (1, place.lat == place.lats - 1)):

        @pl.when(outside)
        def _():
            for grid in grids:
                grid.clear_x(side)

    coupling.clear()
    columns = zone_columns(table_ref)
    finish(loads["zone"])
    for grid in grids:
        grid.fill_props(columns)
    finish(loads["stress"])
    pl.semaphore_wait(barrier, peers)

    turns = [
        Exchange(turn, place, fine, coarse, coupling, turn % 2 == 1, (send_sems, recv_sems))
        for turn in range(2 * STEPS)
    ]

    def open_turn(turn):
        velocity = turn % 2 == 1
        turns[turn].send("head", "corner")

        @pl.when(place.bottom)
        def _():
            coupling.restrict(
                turn,
                fine.velocity if velocity else fine.stress,
                VELOCITY_Z if velocity else STRESS_Z,
            )

        turns[turn].send("lift", "next", "previous", "down", "up")

    def close_turn(turn):
        turns[turn].receive()

        @pl.when(place.bottom)
        def _():
            coupling.interpolate(turn)

        for grid in grids:
            if turn % 2 == 1:
                grid.stress_outer(turn)
            else:
                grid.velocity_outer(turn)

    for step in range(STEPS):
        turn = 2 * step
        open_turn(turn)
        if step == 0:
            finish(loads["velocity"])
        else:
            turns[turn - 1].sent()
        for grid in grids:
            grid.each_row(grid.velocity_inner)
        if step > 0:
            fine.each_row(fine.raise_peak, 0, fine.rows // 2)
        close_turn(turn)
        open_turn(turn + 1)
        if step == 0:
            finish(loads["memory"])
            finish(loads["peak"])
        else:
            fine.each_row(fine.raise_peak, fine.rows // 2)
            coarse.each_row(coarse.raise_peak)
        if step == STEPS - 1:
            start(stores["velocity"])
            start(stores["peak"])
        turns[turn].sent()
        for grid in grids:
            grid.each_row(grid.stress_inner)
        close_turn(turn + 1)
    turns[2 * STEPS - 1].sent()
    start(stores["stress"])
    start(stores["memory"])
    for name in ("velocity", "peak", "stress", "memory"):
        finish(stores[name])


def finish_kernel(table_ref, *refs):
    inputs, outputs = [refs[0:5], refs[5:10]], [refs[10:14], refs[14:18]]
    columns = zone_columns(table_ref)
    tables = strain_tables(columns)
    for (velocity, stress, memory, peak, zone), (new_velocity, new_stress, new_memory, new_peak) in zip(
        inputs, outputs
    ):
        new_velocity[...] = velocity[...]
        new_memory[...] = memory[...]
        rows, _, cells = zone.shape
        for row in range(rows):
            for begin in range(0, cells, LANES):
                lanes = slice(begin, begin + LANES)
                level = zone[row, :, lanes]
                parts = [stress[part, row, :, lanes] for part in range(6)]
                strain = principal(parts, lookup(tables[0], level), lookup(tables[1], level))
                new_peak[row, :, lanes] = jnp.maximum(peak[row, :, lanes], strain)
                for part in range(6):
                    new_stress[part, row, :, lanes] = parts[part]


def shapes_of(velocity, stress, memory, peak):
    return [jax.ShapeDtypeStruct(a.shape, a.dtype) for a in (velocity, stress, memory, peak)]


def scratch_of(peak):
    rows, depth, cells = peak.shape
    tiles, turns = cells // LANES, 2 * STEPS
    full = (tiles, rows + 4, depth + 2 * ROWS, LANES)
    plain = (tiles, rows, depth, LANES)

    def buffer(*shape):
        return pltpu.VMEM(shape, jnp.float32)

    return [
        buffer(6, *full),
        buffer(3, *full),
        buffer(6, *plain),
        buffer(*plain),
        pltpu.VMEM(plain, jnp.int32),
        buffer(7, *plain),
        buffer(turns, 3, tiles, 2, depth, LANES),
        buffer(turns, 3, tiles, 2, depth, LANES),
        buffer(turns, 3, tiles, rows, 3 * ROWS, LANES),
    ]


def on_device(
    velocity_fine,
    stress_fine,
    memory_fine,
    peak_fine,
    zone_fine,
    velocity_coarse,
    stress_coarse,
    memory_coarse,
    peak_coarse,
    zone_coarse,
    zone_table,
    interp_weight,
    restrict_weight,
):
    fine = (velocity_fine, stress_fine, memory_fine, peak_fine)
    coarse = (velocity_coarse, stress_coarse, memory_coarse, peak_coarse)
    fine_rows, _, fine_cells = peak_fine.shape
    coarse_rows, _, coarse_cells = peak_coarse.shape
    block = ROWS * ((coarse_rows + ROWS) // ROWS)
    turns = 2 * STEPS
    hbm = pl.BlockSpec(memory_space=pl.ANY)
    smem = pl.BlockSpec(memory_space=pltpu.SMEM)
    shapes = shapes_of(*fine) + shapes_of(*coarse)
    tiles = fine_cells // LANES + coarse_cells // LANES
    state = pl.pallas_call(
        functools.partial(waves_kernel, None),
        out_shape=shapes,
        in_specs=[smem] * 3 + [hbm] * 10,
        out_specs=[hbm] * 8,
        scratch_shapes=[
            *scratch_of(peak_fine),
            *scratch_of(peak_coarse),
            pltpu.VMEM((turns, 3, 2 * block, coarse_cells), jnp.float32),
            pltpu.VMEM((turns, 3, coarse_cells // LANES, coarse_rows, ROWS, LANES), jnp.float32),
            pltpu.VMEM((3 * coarse_rows * ROWS, fine_cells), jnp.float32),
            pltpu.VMEM((coarse_cells, fine_cells), jnp.float32),
            pltpu.VMEM((fine_cells, coarse_cells), jnp.float32),
            pltpu.SemaphoreType.DMA((5 * tiles,)),
            pltpu.SemaphoreType.DMA((4 * tiles,)),
            pltpu.SemaphoreType.DMA((turns, MESSAGES)),
            pltpu.SemaphoreType.DMA((turns, MESSAGES)),
        ],
        compiler_params=pltpu.CompilerParams(
            collective_id=0, has_side_effects=True, vmem_limit_bytes=60 * 1024 * 1024
        ),
        name="waves",
    )(
        zone_table,
        interp_weight,
        restrict_weight,
        *fine,
        zone_fine,
        *coarse,
        zone_coarse,
    )

    def spec(array, rows):
        lead = array.ndim - 3
        shape = (*array.shape[:lead], rows, *array.shape[lead + 1 :])
        return pl.BlockSpec(shape, lambda i: (*([0] * lead), i, 0, 0))

    steps = coarse_rows
    specs_in, specs_out = [], []
    for grid_shapes, zone, rows in (
        (shapes[:4], zone_fine, fine_rows // steps),
        (shapes[4:], zone_coarse, coarse_rows // steps),
    ):
        specs = [spec(array, rows) for array in grid_shapes]
        specs_in += [*specs, spec(zone, rows)]
        specs_out += specs
    return tuple(
        pl.pallas_call(
            finish_kernel,
            grid=(steps,),
            out_shape=shapes,
            in_specs=[smem, *specs_in],
            out_specs=specs_out,
            compiler_params=pltpu.CompilerParams(vmem_limit_bytes=40 * 1024 * 1024),
            name="finish",
        )(zone_table, *state[:4], zone_fine, *state[4:], zone_coarse)
    )


def solution(mesh):
    field, scalar, whole = P(None, "lat", "depth", None), P("lat", "depth", None), P()
    return jax.shard_map(
        on_device,
        mesh=mesh,
        in_specs=(field, field, field, scalar, scalar) * 2 + (whole,) * 3,
        out_specs=(field, field, field, scalar) * 2,
        check_vma=False,
    )
```

time: 184 us -> 54.1 us (0.29)
  the two profiles are of different devices: /device:TPU:4 before, /device:TPU:27 now
where the time goes in v1:
time: 54.1 us; the launch traced here: 53.6 us
  Pallas kernels  44.1 us (82%)
  local copies, waits for them, and re-layouts  8.84 us (16%)
  between operations  0.71 us (1%)
    pallas_call x1, Pallas kernels, on_device(): pl.pallas_call(functools.partial(waves_kernel, None), out_shape=shapes, i...  38.9 us
    unnamed x22, local copies, waits for them, and re-layouts  8.84 us
    pallas_call x1, Pallas kernels, on_device(): pl.pallas_call(finish_kernel, grid=(steps,), out_shape=shapes, in_specs=[...  5.21 us

profile of v1, /device:TPU:27, one launch (start us, length us, event | category | flops | bytes accessed | tf_op | source)
XLA Modules:
  0.0 53.6 jit_solution(17349533787990294569)
XLA Ops:
  0.6 0.0 copy-start.10
  0.6 0.0 copy-start.7
  0.7 0.0 copy-start.2
  0.7 38.9 %waves.1 = (f32[3,12,16,384]{3,2,1,0:T(8,128)}, f32[6,12,16,384]{3,2,1,0:T(8,128)}, f32[6,12,16,384]{3,2,1,0:T(8,128)}, f32[12,16,384]{2,1,0:T(8,128)}, f32[3,4,...) custom-call(f32[8,5]{1,0:T(8,128)} %table_ref.1, ...), custom_call_target="tpu_custom_call" | custom-call | tf_op jit(solution)/shard_map/waves/pallas_call | solution.py:871
  39.5 0.0 copy-done.10
  39.6 0.0 copy-done.7
  39.6 0.0 copy-done.2
  39.6 0.0 copy-start
  39.6 1.5 %copy-done = f32[6,12,16,384]{3,2,1,0:T(8,128)S(1)} copy-done((f32[6,12,16,384]{3,2,1,0:T(8,128)S(1)}, f32[6,12,16,384]{3,2,1,0:T(8,128)}, u32[]{:S(2)}) %copy-start) | copy-done | bytes 1769496
  41.1 0.0 copy-start.1
  41.1 1.5 %copy-done.1 = f32[6,12,16,384]{3,2,1,0:T(8,128)S(1)} copy-done((f32[6,12,16,384]{3,2,1,0:T(8,128)S(1)}, f32[6,12,16,384]{3,2,1,0:T(8,128)}, u32[]{:S(2)}) %copy-start.1) | copy-done | bytes 1769496
  42.5 0.0 copy-start.3
  42.5 1.2 %copy-done.3 = f32[3,12,16,384]{3,2,1,0:T(8,128)S(1)} copy-done((f32[3,12,16,384]{3,2,1,0:T(8,128)S(1)}, f32[3,12,16,384]{3,2,1,0:T(8,128)}, u32[]{:S(2)}) %copy-start.3) | copy-done | bytes 884760
  43.7 0.0 copy-start.4
  43.7 1.0 %copy-done.4 = f32[6,4,32,128]{3,2,1,0:T(8,128)S(1)} copy-done((f32[6,4,32,128]{3,2,1,0:T(8,128)S(1)}, f32[6,4,32,128]{3,2,1,0:T(8,128)}, u32[]{:S(2)}) %copy-start.4) | copy-done | bytes 393240
  44.7 0.0 copy-start.5
  44.7 1.0 %copy-done.5 = f32[6,4,32,128]{3,2,1,0:T(8,128)S(1)} copy-done((f32[6,4,32,128]{3,2,1,0:T(8,128)S(1)}, f32[6,4,32,128]{3,2,1,0:T(8,128)}, u32[]{:S(2)}) %copy-start.5) | copy-done | bytes 393240
  45.7 0.0 copy-start.6
  45.7 1.0 %copy-done.6 = f32[12,16,384]{2,1,0:T(8,128)S(1)} copy-done((f32[12,16,384]{2,1,0:T(8,128)S(1)}, f32[12,16,384]{2,1,0:T(8,128)}, u32[]{:S(2)}) %copy-start.6) | copy-done | bytes 294936
  46.7 0.0 copy-start.8
  46.7 0.9 %copy-done.8 = f32[3,4,32,128]{3,2,1,0:T(8,128)S(1)} copy-done((f32[3,4,32,128]{3,2,1,0:T(8,128)S(1)}, f32[3,4,32,128]{3,2,1,0:T(8,128)}, u32[]{:S(2)}) %copy-start.8) | copy-done | bytes 196632
  47.6 0.0 copy-start.9
  47.6 0.8 %copy-done.9 = f32[4,32,128]{2,1,0:T(8,128)S(1)} copy-done((f32[4,32,128]{2,1,0:T(8,128)S(1)}, f32[4,32,128]{2,1,0:T(8,128)}, u32[]{:S(2)}) %copy-start.9) | copy-done | bytes 65560
  48.4 5.2 %finish.1 = (f32[3,12,16,384]{3,2,1,0:T(8,128)}, f32[6,12,16,384]{3,2,1,0:T(8,128)}, f32[6,12,16,384]{3,2,1,0:T(8,128)}, f32[12,16,384]{2,1,0:T(8,128)}, f32[3,4...) custom-call(f32[8,5]{1,0:T(8,128)S(1)} %copy-done.10, ...), custom_call_target="tpu_custom_call" | custom-call | tf_op jit(solution)/shard_map/finish/pallas_call | solution.py:918
Async XLA Ops:
  0.6 38.9 %copy-start.10 = (f32[8,5]{1,0:T(8,128)S(1)}, f32[8,5]{1,0:T(8,128)}, u32[]{:S(2)}) copy-start(f32[8,5]{1,0:T(8,128)} %table_ref.1) | copy-start | bytes 484
  0.6 38.9 %copy-start.7 = (s32[4,32,128]{2,1,0:T(8,128)S(1)}, s32[4,32,128]{2,1,0:T(8,128)}, u32[]{:S(2)}) copy-start(s32[4,32,128]{2,1,0:T(8,128)} %refs_9_.3) | copy-start | bytes 196612
  0.7 38.9 %copy-start.2 = (s32[12,16,384]{2,1,0:T(8,128)S(1)}, s32[12,16,384]{2,1,0:T(8,128)}, u32[]{:S(2)}) copy-start(s32[12,16,384]{2,1,0:T(8,128)} %refs_4_.3) | copy-start | bytes 884740
  39.6 1.5 %copy-start = (f32[6,12,16,384]{3,2,1,0:T(8,128)S(1)}, f32[6,12,16,384]{3,2,1,0:T(8,128)}, u32[]{:S(2)}) copy-start(f32[6,12,16,384]{3,2,1,0:T(8,128)} %get-tuple-element.17.refs_1_) | copy-start | bytes 5308420
  41.1 1.5 %copy-start.1 = (f32[6,12,16,384]{3,2,1,0:T(8,128)S(1)}, f32[6,12,16,384]{3,2,1,0:T(8,128)}, u32[]{:S(2)}) copy-start(f32[6,12,16,384]{3,2,1,0:T(8,128)} %get-tuple-element.18.refs_2_) | copy-start | bytes 5308420
  42.5 1.2 %copy-start.3 = (f32[3,12,16,384]{3,2,1,0:T(8,128)S(1)}, f32[3,12,16,384]{3,2,1,0:T(8,128)}, u32[]{:S(2)}) copy-start(f32[3,12,16,384]{3,2,1,0:T(8,128)} %get-tuple-element.16.refs_0_) | copy-start | bytes 2654212
  43.7 1.0 %copy-start.4 = (f32[6,4,32,128]{3,2,1,0:T(8,128)S(1)}, f32[6,4,32,128]{3,2,1,0:T(8,128)}, u32[]{:S(2)}) copy-start(f32[6,4,32,128]{3,2,1,0:T(8,128)} %get-tuple-element.21.refs_6_) | copy-start | bytes 1179652
  44.7 1.0 %copy-start.5 = (f32[6,4,32,128]{3,2,1,0:T(8,128)S(1)}, f32[6,4,32,128]{3,2,1,0:T(8,128)}, u32[]{:S(2)}) copy-start(f32[6,4,32,128]{3,2,1,0:T(8,128)} %get-tuple-element.22.refs_7_) | copy-start | bytes 1179652
  45.7 1.0 %copy-start.6 = (f32[12,16,384]{2,1,0:T(8,128)S(1)}, f32[12,16,384]{2,1,0:T(8,128)}, u32[]{:S(2)}) copy-start(f32[12,16,384]{2,1,0:T(8,128)} %get-tuple-element.19.refs_3_) | copy-start | bytes 884740
  46.7 0.9 %copy-start.8 = (f32[3,4,32,128]{3,2,1,0:T(8,128)S(1)}, f32[3,4,32,128]{3,2,1,0:T(8,128)}, u32[]{:S(2)}) copy-start(f32[3,4,32,128]{3,2,1,0:T(8,128)} %get-tuple-element.20.refs_5_) | copy-start | bytes 589828
  47.6 0.8 %copy-start.9 = (f32[4,32,128]{2,1,0:T(8,128)S(1)}, f32[4,32,128]{2,1,0:T(8,128)}, u32[]{:S(2)}) copy-start(f32[4,32,128]{2,1,0:T(8,128)} %get-tuple-element.23.refs_8_) | copy-start | bytes 196612

commit v2 on v1

--- a/solution.py
+++ b/solution.py
@@ -144,8 +144,8 @@
             self.velocity,
             self.memory,
             self.peak,
+            self.props,
             self.zone,
-            self.props,
             self.below_x,
             self.above_x,
             self.around_z,
@@ -279,13 +279,16 @@
     def ends(self):
         return (0, self.depth - ROWS)
 
-    def velocity_outer(self, turn):
+    def velocity_outer_x(self, turn):
         velocity, depth = self.velocity, self.depth
         for part in range(3):
             for tile in range(self.tiles):
                 for row, term in self.outer_rows(turn, part, tile, STRESS_X[part][1]):
                     place = velocity.at[part, tile, row + 2, pl.ds(ROWS, depth), :]
                     place[...] = place[...] + self.props[BUOYANCY, tile, row] * term
+
+    def velocity_outer_z(self, turn):
+        velocity = self.velocity
 
         def body(row):
             for part in range(3):
@@ -355,7 +358,7 @@
         shear = self.props[SHEAR, tile, row, pl.ds(begin, count), :]
         return [(part, (0.5 * shear) * term)]
 
-    def stress_outer(self, turn):
+    def stress_outer_x(self, turn):
         depth = self.depth
         for tile in range(self.tiles):
             for row, term in self.outer_rows(turn, 0, tile, BACKWARD):
@@ -366,6 +369,7 @@
                     rates = self.shear_rates(term, part, tile, row, 0, depth)
                     self.add_rates(rates, tile, row, 0, depth)
 
+    def stress_outer_z(self, turn):
         def body(row):
             for tile in range(self.tiles):
                 normal = self.outer_layers(turn, 2, tile, row, BACKWARD)
@@ -636,9 +640,10 @@
 
 
 MESSAGES = 64
-
-
-def waves_kernel(counts, *refs):
+KERNEL_BYTES = 32 * 1024 * 1024
+
+
+def waves_kernel(*refs):
     refs = list(refs)
 
     def take(count):
@@ -648,97 +653,51 @@
 
     table_ref, interp_ref, restrict_ref = take(3)
     inputs = [take(5), take(5)]
-    outputs = [take(4), take(4)]
-    fine, coarse = Field(1.0, take(9)), Field(3.0, take(9))
+    states = [take(5), take(5)]
+    fine = Field(1.0, states[0] + take(4))
+    coarse = Field(3.0, states[1] + take(4))
     coupling = Coupling(fine, coarse, interp_ref, restrict_ref, take(5))
-    load_sems, store_sems, send_sems, recv_sems = take(4)
+    load_sems, send_sems, recv_sems = take(3)
     place = Place()
     grids = (fine, coarse)
 
-    loads, stores = {}, {}
+    loads, count = {}, 0
     for grid, (velocity, stress, memory, peak, zone) in zip(grids, inputs):
-        inner_rows, inner = pl.ds(2, grid.rows), pl.ds(ROWS, grid.depth)
-        pairs = [
-            ("zone", zone, grid.zone, None),
-            ("stress", stress, grid.stress, inner),
-            ("velocity", velocity, grid.velocity, inner),
-            ("memory", memory, grid.memory, None),
-            ("peak", peak, grid.peak, None),
-        ]
-        for name, source, target, padded in pairs:
-            for tile in range(grid.tiles):
-                lanes = pl.ds(tile * LANES, LANES)
-                if name in ("zone", "peak"):
-                    source_part, target_part = source.at[:, :, lanes], target.at[tile]
-                elif padded is None:
-                    source_part, target_part = source.at[:, :, :, lanes], target.at[:, tile]
-                else:
-                    source_part = source.at[:, :, :, lanes]
-                    target_part = target.at[:, tile, inner_rows, padded, :]
-                index = sum(len(group) for group in loads.values())
-                copy = pltpu.make_async_copy(source_part, target_part, load_sems.at[index])
-                loads.setdefault(name, []).append(copy)
-    for grid, (velocity, stress, memory, peak) in zip(grids, outputs):
-        inner_rows, inner = pl.ds(2, grid.rows), pl.ds(ROWS, grid.depth)
+        rows, inner = pl.ds(2, grid.rows), pl.ds(ROWS, grid.depth)
         for tile in range(grid.tiles):
             lanes = pl.ds(tile * LANES, LANES)
-            for name, source_part, target_part in (
-                ("velocity", grid.velocity.at[:, tile, inner_rows, inner, :], velocity.at[:, :, :, lanes]),
-                ("stress", grid.stress.at[:, tile, inner_rows, inner, :], stress.at[:, :, :, lanes]),
-                ("memory", grid.memory.at[:, tile], memory.at[:, :, :, lanes]),
-                ("peak", grid.peak.at[tile], peak.at[:, :, lanes]),
+            for name, source, target in (
+                ("zone", zone.at[:, :, lanes], grid.zone.at[tile]),
+                ("stress", stress.at[:, :, :, lanes], grid.stress.at[:, tile, rows, inner, :]),
+                ("velocity", velocity.at[:, :, :, lanes], grid.velocity.at[:, tile, rows, inner, :]),
+                ("memory", memory.at[:, :, :, lanes], grid.memory.at[:, tile]),
+                ("peak", peak.at[:, :, lanes], grid.peak.at[tile]),
             ):
-                index = sum(len(group) for group in stores.values())
-                copy = pltpu.make_async_copy(source_part, target_part, store_sems.at[index])
-                stores.setdefault(name, []).append(copy)
-
-    def start(group):
-        for copy in group:
+                copy = pltpu.make_async_copy(source, target, load_sems.at[count])
+                loads.setdefault(name, []).append(copy)
+                count += 1
+
+    def start(name):
+        for copy in loads[name]:
             copy.start()
 
-    def finish(group):
-        for copy in group:
+    def finish(name):
+        for copy in loads[name]:
             copy.wait()
 
-    for name in ("zone", "stress", "velocity", "memory", "peak"):
-        start(loads[name])
+    start("stress")
     coupling.heads[...] = jnp.zeros(coupling.heads.shape, jnp.float32)
     barrier, peers = place.greet()
-
-    for grid in grids:
-        grid.clear()
-
-    @pl.when(place.top)
-    def _():
-        fine.clear_z(0)
-
-    @pl.when(place.bottom)
-    def _():
-        coarse.clear_z(1)
-
-    for side, outside in ((0, place.lat == 0), (1, place.lat == place.lats - 1)):
-
-        @pl.when(outside)
-        def _():
-            for grid in grids:
-                grid.clear_x(side)
-
-    coupling.clear()
-    columns = zone_columns(table_ref)
-    finish(loads["zone"])
-    for grid in grids:
-        grid.fill_props(columns)
-    finish(loads["stress"])
-    pl.semaphore_wait(barrier, peers)
+    for name in ("zone", "velocity", "memory", "peak"):
+        start(name)
 
     turns = [
         Exchange(turn, place, fine, coarse, coupling, turn % 2 == 1, (send_sems, recv_sems))
         for turn in range(2 * STEPS)
     ]
 
-    def open_turn(turn):
+    def restrict(turn):
         velocity = turn % 2 == 1
-        turns[turn].send("head", "corner")
 
         @pl.when(place.bottom)
         def _():
@@ -748,26 +707,64 @@
                 VELOCITY_Z if velocity else STRESS_Z,
             )
 
-        turns[turn].send("lift", "next", "previous", "down", "up")
+        turns[turn].send("lift")
+
+    def open_turn(turn):
+        turns[turn].send("head", "corner", "next", "previous", "down", "up")
 
     def close_turn(turn):
-        turns[turn].receive()
+        turns[turn].receive("head", "corner")
 
         @pl.when(place.bottom)
         def _():
             coupling.interpolate(turn)
 
+        turns[turn].receive("down", "up", "lift")
         for grid in grids:
             if turn % 2 == 1:
-                grid.stress_outer(turn)
+                grid.stress_outer_z(turn)
             else:
-                grid.velocity_outer(turn)
+                grid.velocity_outer_z(turn)
+        turns[turn].receive("next", "previous")
+        for grid in grids:
+            if turn % 2 == 1:
+                grid.stress_outer_x(turn)
+            else:
+                grid.velocity_outer_x(turn)
+
+    finish("stress")
+    pl.semaphore_wait(barrier, peers)
+    open_turn(0)
+    coupling.clear()
+    restrict(0)
+
+    for grid in grids:
+        grid.clear()
+
+    @pl.when(place.top)
+    def _():
+        fine.clear_z(0)
+
+    @pl.when(place.bottom)
+    def _():
+        coarse.clear_z(1)
+
+    for side, outside in ((0, place.lat == 0), (1, place.lat == place.lats - 1)):
+
+        @pl.when(outside)
+        def _():
+            for grid in grids:
+                grid.clear_x(side)
+
+    columns = zone_columns(table_ref)
+    finish("zone")
+    for grid in grids:
+        grid.fill_props(columns)
 
     for step in range(STEPS):
         turn = 2 * step
-        open_turn(turn)
         if step == 0:
-            finish(loads["velocity"])
+            finish("velocity")
         else:
             turns[turn - 1].sent()
         for grid in grids:
@@ -776,71 +773,86 @@
             fine.each_row(fine.raise_peak, 0, fine.rows // 2)
         close_turn(turn)
         open_turn(turn + 1)
+        restrict(turn + 1)
         if step == 0:
-            finish(loads["memory"])
-            finish(loads["peak"])
+            finish("memory")
+            finish("peak")
         else:
             fine.each_row(fine.raise_peak, fine.rows // 2)
             coarse.each_row(coarse.raise_peak)
-        if step == STEPS - 1:
-            start(stores["velocity"])
-            start(stores["peak"])
         turns[turn].sent()
         for grid in grids:
             grid.each_row(grid.stress_inner)
         close_turn(turn + 1)
+        if step < STEPS - 1:
+            open_turn(turn + 2)
+            restrict(turn + 2)
     turns[2 * STEPS - 1].sent()
-    start(stores["stress"])
-    start(stores["memory"])
-    for name in ("velocity", "peak", "stress", "memory"):
-        finish(stores[name])
-
-
-def finish_kernel(table_ref, *refs):
-    inputs, outputs = [refs[0:5], refs[5:10]], [refs[10:14], refs[14:18]]
-    columns = zone_columns(table_ref)
-    tables = strain_tables(columns)
-    for (velocity, stress, memory, peak, zone), (new_velocity, new_stress, new_memory, new_peak) in zip(
-        inputs, outputs
+
+
+def finish_kernel(*refs):
+    states, outputs = [refs[0:5], refs[5:10]], [refs[10:14], refs[14:18]]
+    peaks, sems = refs[18:20], refs[20]
+    copies, count = [], 0
+
+    def move(source, target):
+        nonlocal count
+        copy = pltpu.make_async_copy(source, target, sems.at[count])
+        copy.start()
+        copies.append(copy)
+        count += 1
+
+    for (stress, velocity, memory, peak, _), (new_velocity, new_stress, new_memory, _) in zip(
+        states, outputs
     ):
-        new_velocity[...] = velocity[...]
-        new_memory[...] = memory[...]
-        rows, _, cells = zone.shape
-        for row in range(rows):
-            for begin in range(0, cells, LANES):
-                lanes = slice(begin, begin + LANES)
-                level = zone[row, :, lanes]
-                parts = [stress[part, row, :, lanes] for part in range(6)]
-                strain = principal(parts, lookup(tables[0], level), lookup(tables[1], level))
-                new_peak[row, :, lanes] = jnp.maximum(peak[row, :, lanes], strain)
-                for part in range(6):
-                    new_stress[part, row, :, lanes] = parts[part]
-
-
-def shapes_of(velocity, stress, memory, peak):
-    return [jax.ShapeDtypeStruct(a.shape, a.dtype) for a in (velocity, stress, memory, peak)]
+        tiles, rows, depth, _ = peak.shape
+        inner_rows, inner = pl.ds(2, rows), pl.ds(ROWS, depth)
+        for tile in range(tiles):
+            lanes = pl.ds(tile * LANES, LANES)
+            move(stress.at[:, tile, inner_rows, inner, :], new_stress.at[:, :, :, lanes])
+            move(memory.at[:, tile], new_memory.at[:, :, :, lanes])
+            move(velocity.at[:, tile, inner_rows, inner, :], new_velocity.at[:, :, :, lanes])
+    for (stress, _, _, peak, props), (_, _, _, new_peak), raised in zip(states, outputs, peaks):
+        tiles, rows, depth, _ = peak.shape
+        half = rows // 2
+
+        def body(row, carry):
+            for tile in range(tiles):
+                strain = principal(
+                    [stress[part, tile, row + 2, pl.ds(ROWS, depth), :] for part in range(6)],
+                    props[VOLUMETRIC, tile, row],
+                    props[SCALE, tile, row],
+                )
+                raised[tile, row] = jnp.maximum(peak[tile, row], strain)
+            return carry
+
+        for begin, end in ((0, half), (half, rows)):
+            lax.fori_loop(begin, end, body, 0)
+            span = pl.ds(begin, end - begin)
+            for tile in range(tiles):
+                move(raised.at[tile, span], new_peak.at[span, :, pl.ds(tile * LANES, LANES)])
+    for copy in copies:
+        copy.wait()
+
+
+def sizes_of(peak):
+    rows, depth, cells = peak.shape
+    tiles = cells // LANES
+    return tiles, (tiles, rows + 4, depth + 2 * ROWS, LANES), (tiles, rows, depth, LANES)
+
+
+def state_of(peak):
+    _, full, plain = sizes_of(peak)
+    shapes = [(6, *full), (3, *full), (6, *plain), plain, (7, *plain)]
+    return [pltpu.VMEM(shape, jnp.float32) for shape in shapes]
 
 
 def scratch_of(peak):
-    rows, depth, cells = peak.shape
-    tiles, turns = cells // LANES, 2 * STEPS
-    full = (tiles, rows + 4, depth + 2 * ROWS, LANES)
-    plain = (tiles, rows, depth, LANES)
-
-    def buffer(*shape):
-        return pltpu.VMEM(shape, jnp.float32)
-
-    return [
-        buffer(6, *full),
-        buffer(3, *full),
-        buffer(6, *plain),
-        buffer(*plain),
-        pltpu.VMEM(plain, jnp.int32),
-        buffer(7, *plain),
-        buffer(turns, 3, tiles, 2, depth, LANES),
-        buffer(turns, 3, tiles, 2, depth, LANES),
-        buffer(turns, 3, tiles, rows, 3 * ROWS, LANES),
-    ]
+    tiles, _, plain = sizes_of(peak)
+    _, rows, depth, _ = plain
+    side = pltpu.VMEM((2 * STEPS, 3, tiles, 2, depth, LANES), jnp.float32)
+    around = pltpu.VMEM((2 * STEPS, 3, tiles, rows, 3 * ROWS, LANES), jnp.float32)
+    return [pltpu.VMEM(plain, jnp.int32), side, side, around]
 
 
 def on_device(
@@ -866,13 +878,13 @@
     turns = 2 * STEPS
     hbm = pl.BlockSpec(memory_space=pl.ANY)
     smem = pl.BlockSpec(memory_space=pltpu.SMEM)
-    shapes = shapes_of(*fine) + shapes_of(*coarse)
+    vmem = pl.BlockSpec(memory_space=pltpu.VMEM)
     tiles = fine_cells // LANES + coarse_cells // LANES
     state = pl.pallas_call(
-        functools.partial(waves_kernel, None),
-        out_shape=shapes,
+        waves_kernel,
+        out_shape=state_of(peak_fine) + state_of(peak_coarse),
         in_specs=[smem] * 3 + [hbm] * 10,
-        out_specs=[hbm] * 8,
+        out_specs=[vmem] * 10,
         scratch_shapes=[
             *scratch_of(peak_fine),
             *scratch_of(peak_coarse),
@@ -882,48 +894,42 @@
             pltpu.VMEM((coarse_cells, fine_cells), jnp.float32),
             pltpu.VMEM((fine_cells, coarse_cells), jnp.float32),
             pltpu.SemaphoreType.DMA((5 * tiles,)),
-            pltpu.SemaphoreType.DMA((4 * tiles,)),
             pltpu.SemaphoreType.DMA((turns, MESSAGES)),
             pltpu.SemaphoreType.DMA((turns, MESSAGES)),
         ],
         compiler_params=pltpu.CompilerParams(
-            collective_id=0, has_side_effects=True, vmem_limit_bytes=60 * 1024 * 1024
+            collective_id=0, has_side_effects=True, vmem_limit_bytes=KERNEL_BYTES
         ),
         name="waves",
     )(
-        zone_table,
-        interp_weight,
-        restrict_weight,
-        *fine,
-        zone_fine,
-        *coarse,
-        zone_coarse,
+        *(
+            pltpu.with_memory_space_constraint(array, pltpu.HBM)
+            for array in (
+                zone_table,
+                interp_weight,
+                restrict_weight,
+                *fine,
+                zone_fine,
+                *coarse,
+                zone_coarse,
+            )
+        )
     )
-
-    def spec(array, rows):
-        lead = array.ndim - 3
-        shape = (*array.shape[:lead], rows, *array.shape[lead + 1 :])
-        return pl.BlockSpec(shape, lambda i: (*([0] * lead), i, 0, 0))
-
-    steps = coarse_rows
-    specs_in, specs_out = [], []
-    for grid_shapes, zone, rows in (
-        (shapes[:4], zone_fine, fine_rows // steps),
-        (shapes[4:], zone_coarse, coarse_rows // steps),
-    ):
-        specs = [spec(array, rows) for array in grid_shapes]
-        specs_in += [*specs, spec(zone, rows)]
-        specs_out += specs
+    outputs = (*fine, *coarse)
     return tuple(
         pl.pallas_call(
             finish_kernel,
-            grid=(steps,),
-            out_shape=shapes,
-            in_specs=[smem, *specs_in],
-            out_specs=specs_out,
-            compiler_params=pltpu.CompilerParams(vmem_limit_bytes=40 * 1024 * 1024),
+            out_shape=[jax.ShapeDtypeStruct(array.shape, array.dtype) for array in outputs],
+            in_specs=[vmem] * 10,
+            out_specs=[hbm] * 8,
+            scratch_shapes=[
+                pltpu.VMEM(sizes_of(peak_fine)[2], jnp.float32),
+                pltpu.VMEM(sizes_of(peak_coarse)[2], jnp.float32),
+                pltpu.SemaphoreType.DMA((5 * tiles,)),
+            ],
+            compiler_params=pltpu.CompilerParams(vmem_limit_bytes=KERNEL_BYTES),
             name="finish",
-        )(zone_table, *state[:4], zone_fine, *state[4:], zone_coarse)
+        )(*state)
     )
 
 

time: 54.1 us -> 40 us (0.74)
  the two profiles are of different devices: /device:TPU:27 before, /device:TPU:1 now
where the time goes in v2:
time: 40 us; the launch traced here: 39.8 us
  Pallas kernels  39.2 us (98%)
  between operations  0.65 us (2%)
    pallas_call x1, Pallas kernels, on_device(): pl.pallas_call(waves_kernel, out_shape=state_of(peak_fine) + state_of(pea...  34.6 us
    pallas_call x1, Pallas kernels, on_device(): pl.pallas_call(finish_kernel, out_shape=[jax.ShapeDtypeStruct(array.shape...  4.62 us

profile of v2, /device:TPU:1, one launch (start us, length us, event | category | flops | bytes accessed | tf_op | source)
XLA Modules:
  0.0 39.8 jit_solution(8904335547888694439)
XLA Ops:
  0.6 34.6 %waves.1 = (f32[6,3,16,32,128]{4,3,2,1,0:T(8,128)S(1)}, f32[3,3,16,32,128]{4,3,2,1,0:T(8,128)S(1)}, f32[6,3,12,16,128]{4,3,2,1,0:T(8,128)S(1)}, f32[3,12,16,128]...) custom-call(f32[8,5]{1,0:T(8,128)} %refs_0_.1, ...), custom_call_target="tpu_custom_call" | custom-call | tf_op jit(solution)/shard_map/waves/pallas_call | solution.py:883
  35.2 4.6 %finish.1 = (f32[3,12,16,384]{3,2,1,0:T(8,128)}, f32[6,12,16,384]{3,2,1,0:T(8,128)}, f32[6,12,16,384]{3,2,1,0:T(8,128)}, f32[12,16,384]{2,1,0:T(8,128)}, f32[3,4...) custom-call(f32[6,3,16,32,128]{4,3,2,1,0:T(8,128)S(1)} %get-tuple-element.18., ...), custom_call_target="tpu_custom_call" | custom-call | tf_op jit(solution)/shard_map/finish/pallas_call | solution.py:920

commit v3 on v2

--- a/solution.py
+++ b/solution.py
@@ -1,4 +1,4 @@
-import functools
+import math
 
 import jax
 import jax.numpy as jnp
@@ -29,41 +29,32 @@
 EXACT = lax.Precision.HIGHEST
 
 
-def zone_columns(table_ref):
-    lane = lax.broadcasted_iota(jnp.int32, (ROWS, LANES), 1)
-    columns = []
-    for column in range(table_ref.shape[1]):
-        value = jnp.full((ROWS, LANES), table_ref[0, column], jnp.float32)
-        for level in range(1, table_ref.shape[0]):
-            value = jnp.where(lane == level, table_ref[level, column], value)
-        columns.append(value)
-    return columns
-
-
-def strain_tables(columns):
-    lame, shear = columns[1], columns[2]
-    return [lame / (3.0 * lame + 2.0 * shear), 0.5 / shear]
-
-
-def step_tables(columns, spacing):
-    buoyancy, lame, shear, decay, damping = columns
-    return [
-        buoyancy * (TIME_STEP * NEAR / spacing),
-        lame * (NEAR / spacing),
-        shear * (2.0 * NEAR / spacing),
-        decay,
-        damping * (1.0 - decay),
-    ]
-
-
-def lookup(table, zone):
-    parts = [
-        jnp.take_along_axis(
-            table, zone[begin : begin + ROWS], axis=1, mode="promise_in_bounds"
+def property_tables(table_ref, spacing):
+    def fill(column, level):
+        return jnp.full((ROWS, LANES), table_ref[level, column], jnp.float32)
+
+    tables = []
+    for level in range(table_ref.shape[0]):
+        buoyancy, lame, shear, decay, damping = (fill(column, level) for column in range(5))
+        tables.append(
+            [
+                buoyancy * (TIME_STEP * NEAR / spacing),
+                lame * (NEAR / spacing),
+                shear * (2.0 * NEAR / spacing),
+                decay,
+                damping * (1.0 - decay),
+                lame / (3.0 * lame + 2.0 * shear),
+                0.5 / shear,
+            ]
         )
-        for begin in range(0, zone.shape[0], ROWS)
-    ]
-    return jnp.concatenate(parts, axis=0)
+    return tables
+
+
+def select(masks, values):
+    for mask in masks:
+        pairs = [values[i : i + 2] for i in range(0, len(values), 2)]
+        values = [jnp.where(mask, pair[-1], pair[0]) for pair in pairs]
+    return values[0]
 
 
 def rotation(low, high, pivot):
@@ -218,14 +209,22 @@
 
         self.each_row(body)
 
-    def fill_props(self, columns):
-        tables = step_tables(columns, self.spacing) + strain_tables(columns)
+    def fill_props(self, table_ref, filled):
+        zones = table_ref.shape[0]
+        for level, values in enumerate(property_tables(table_ref, self.spacing)):
+            for index, value in enumerate(values):
+                filled[index, level] = value
 
         def body(row):
             for tile in range(self.tiles):
-                zone = self.zone[tile, row]
-                for index, table in enumerate(tables):
-                    self.props[index, tile, row] = lookup(table, zone)
+                for begin in range(0, self.depth, ROWS):
+                    zone = self.zone[tile, row, begin : begin + ROWS, :]
+                    masks = [
+                        jnp.bitwise_and(zone, 1 << bit) != 0 for bit in range((zones - 1).bit_length())
+                    ]
+                    for index in range(filled.shape[0]):
+                        values = [filled[index, level] for level in range(zones)]
+                        self.props[index, tile, row, begin : begin + ROWS, :] = select(masks, values)
 
         self.each_row(body)
 
@@ -551,7 +550,9 @@
         along_x = VELOCITY_X if velocity else STRESS_X
         along_z = VELOCITY_Z if velocity else STRESS_Z
         self.messages = {route: [] for route in place.routes}
-        self.send_sems, self.recv_sems, self.count, self.turn = sems[0], sems[1], 0, turn
+        self.numbers = {route: number for number, route in enumerate(place.routes)}
+        self.length = dict.fromkeys(place.routes, 0)
+        self.send_sems, self.recv_sems, self.token = (sems[0].at[turn], sems[1].at[turn], sems[2])
         ref = coarse.velocity if velocity else coarse.stress
         block = coupling.block
         for slot, (part, (low, _)) in enumerate(along_z):
@@ -603,19 +604,24 @@
                 )
 
     def add(self, route, source, target):
+        number = self.numbers[route]
         copy = pltpu.make_async_remote_copy(
             src_ref=source,
             dst_ref=target,
-            send_sem=self.send_sems.at[self.turn, self.count],
-            recv_sem=self.recv_sems.at[self.turn, self.count],
+            send_sem=self.send_sems.at[number],
+            recv_sem=self.recv_sems.at[number],
             device_id=self.place.target(route),
             device_id_type=MESH,
         )
         self.messages[route].append(copy)
-        self.count += 1
+        self.length[route] += math.prod(target.shape) // LANES
+
+    def settle(self, route, sem):
+        whole = self.token.at[pl.ds(0, self.length[route]), :]
+        pltpu.make_async_copy(whole, whole, sem).wait()
 
     def send(self, *routes):
-        for route in routes or self.messages:
+        for route in routes:
 
             @pl.when(self.place.routes[route][2])
             def _():
@@ -623,23 +629,21 @@
                     copy.start()
 
     def receive(self, *routes):
-        for route in routes or self.messages:
+        for route in routes:
 
             @pl.when(self.place.routes[route][3])
             def _():
-                for copy in self.messages[route]:
-                    copy.wait_recv()
+                self.settle(route, self.recv_sems.at[self.numbers[route]])
 
     def sent(self):
         for route in self.messages:
 
             @pl.when(self.place.routes[route][2])
             def _():
-                for copy in self.messages[route]:
-                    copy.wait_send()
-
-
-MESSAGES = 64
+                self.settle(route, self.send_sems.at[self.numbers[route]])
+
+
+ROUTES = 7
 KERNEL_BYTES = 32 * 1024 * 1024
 
 
@@ -657,33 +661,42 @@
     fine = Field(1.0, states[0] + take(4))
     coarse = Field(3.0, states[1] + take(4))
     coupling = Coupling(fine, coarse, interp_ref, restrict_ref, take(5))
+    filled, token = take(2)
     load_sems, send_sems, recv_sems = take(3)
     place = Place()
     grids = (fine, coarse)
 
-    loads, count = {}, 0
-    for grid, (velocity, stress, memory, peak, zone) in zip(grids, inputs):
+    loads = {}
+    for grid, arrays, sems in zip(grids, inputs, (load_sems.at[0], load_sems.at[1])):
+        velocity, stress, memory, peak, zone = arrays
         rows, inner = pl.ds(2, grid.rows), pl.ds(ROWS, grid.depth)
-        for tile in range(grid.tiles):
-            lanes = pl.ds(tile * LANES, LANES)
-            for name, source, target in (
-                ("zone", zone.at[:, :, lanes], grid.zone.at[tile]),
-                ("stress", stress.at[:, :, :, lanes], grid.stress.at[:, tile, rows, inner, :]),
-                ("velocity", velocity.at[:, :, :, lanes], grid.velocity.at[:, tile, rows, inner, :]),
-                ("memory", memory.at[:, :, :, lanes], grid.memory.at[:, tile]),
-                ("peak", peak.at[:, :, lanes], grid.peak.at[tile]),
-            ):
-                copy = pltpu.make_async_copy(source, target, load_sems.at[count])
-                loads.setdefault(name, []).append(copy)
-                count += 1
+        wholes = (zone, stress, velocity, memory, peak)
+        for index, name in enumerate(("zone", "stress", "velocity", "memory", "peak")):
+            copies = []
+            for tile in range(grid.tiles):
+                lanes = pl.ds(tile * LANES, LANES)
+                source, target = {
+                    "zone": (zone.at[:, :, lanes], grid.zone.at[tile]),
+                    "stress": (stress.at[:, :, :, lanes], grid.stress.at[:, tile, rows, inner, :]),
+                    "velocity": (
+                        velocity.at[:, :, :, lanes],
+                        grid.velocity.at[:, tile, rows, inner, :],
+                    ),
+                    "memory": (memory.at[:, :, :, lanes], grid.memory.at[:, tile]),
+                    "peak": (peak.at[:, :, lanes], grid.peak.at[tile]),
+                }[name]
+                copies.append(pltpu.make_async_copy(source, target, sems.at[index]))
+            whole = pltpu.make_async_copy(wholes[index], wholes[index], sems.at[index])
+            loads.setdefault(name, []).append((copies, whole))
 
     def start(name):
-        for copy in loads[name]:
-            copy.start()
+        for copies, _ in loads[name]:
+            for copy in copies:
+                copy.start()
 
     def finish(name):
-        for copy in loads[name]:
-            copy.wait()
+        for _, whole in loads[name]:
+            whole.wait()
 
     start("stress")
     coupling.heads[...] = jnp.zeros(coupling.heads.shape, jnp.float32)
@@ -692,7 +705,7 @@
         start(name)
 
     turns = [
-        Exchange(turn, place, fine, coarse, coupling, turn % 2 == 1, (send_sems, recv_sems))
+        Exchange(turn, place, fine, coarse, coupling, turn % 2 == 1, (send_sems, recv_sems, token))
         for turn in range(2 * STEPS)
     ]
 
@@ -756,10 +769,9 @@
             for grid in grids:
                 grid.clear_x(side)
 
-    columns = zone_columns(table_ref)
     finish("zone")
     for grid in grids:
-        grid.fill_props(columns)
+        grid.fill_props(table_ref, filled)
 
     for step in range(STEPS):
         turn = 2 * step
@@ -793,26 +805,26 @@
 def finish_kernel(*refs):
     states, outputs = [refs[0:5], refs[5:10]], [refs[10:14], refs[14:18]]
     peaks, sems = refs[18:20], refs[20]
-    copies, count = [], 0
-
-    def move(source, target):
-        nonlocal count
-        copy = pltpu.make_async_copy(source, target, sems.at[count])
-        copy.start()
-        copies.append(copy)
-        count += 1
-
-    for (stress, velocity, memory, peak, _), (new_velocity, new_stress, new_memory, _) in zip(
-        states, outputs
-    ):
+    wholes = []
+    for grid, ((stress, velocity, memory, peak, _), arrays) in enumerate(zip(states, outputs)):
+        new_velocity, new_stress, new_memory, _ = arrays
         tiles, rows, depth, _ = peak.shape
         inner_rows, inner = pl.ds(2, rows), pl.ds(ROWS, depth)
         for tile in range(tiles):
             lanes = pl.ds(tile * LANES, LANES)
-            move(stress.at[:, tile, inner_rows, inner, :], new_stress.at[:, :, :, lanes])
-            move(memory.at[:, tile], new_memory.at[:, :, :, lanes])
-            move(velocity.at[:, tile, inner_rows, inner, :], new_velocity.at[:, :, :, lanes])
-    for (stress, _, _, peak, props), (_, _, _, new_peak), raised in zip(states, outputs, peaks):
+            for index, (source, target) in enumerate(
+                (
+                    (velocity.at[:, tile, inner_rows, inner, :], new_velocity),
+                    (stress.at[:, tile, inner_rows, inner, :], new_stress),
+                    (memory.at[:, tile], new_memory),
+                )
+            ):
+                place = target.at[:, :, :, lanes]
+                pltpu.make_async_copy(source, place, sems.at[grid, index]).start()
+        wholes += [(array, sems.at[grid, index]) for index, array in enumerate(arrays)]
+    for grid, ((stress, _, _, peak, props), (_, _, _, new_peak), raised) in enumerate(
+        zip(states, outputs, peaks)
+    ):
         tiles, rows, depth, _ = peak.shape
         half = rows // 2
 
@@ -830,9 +842,10 @@
             lax.fori_loop(begin, end, body, 0)
             span = pl.ds(begin, end - begin)
             for tile in range(tiles):
-                move(raised.at[tile, span], new_peak.at[span, :, pl.ds(tile * LANES, LANES)])
-    for copy in copies:
-        copy.wait()
+                place = new_peak.at[span, :, pl.ds(tile * LANES, LANES)]
+                pltpu.make_async_copy(raised.at[tile, span], place, sems.at[grid, 3]).start()
+    for array, sem in wholes:
+        pltpu.make_async_copy(array, array, sem).wait()
 
 
 def sizes_of(peak):
@@ -879,7 +892,9 @@
     hbm = pl.BlockSpec(memory_space=pl.ANY)
     smem = pl.BlockSpec(memory_space=pltpu.SMEM)
     vmem = pl.BlockSpec(memory_space=pltpu.VMEM)
-    tiles = fine_cells // LANES + coarse_cells // LANES
+    token_rows = sum(
+        5 * (peak.size // LANES) // min(peak.shape[:2]) for peak in (peak_fine, peak_coarse)
+    )
     state = pl.pallas_call(
         waves_kernel,
         out_shape=state_of(peak_fine) + state_of(peak_coarse),
@@ -893,9 +908,11 @@
             pltpu.VMEM((3 * coarse_rows * ROWS, fine_cells), jnp.float32),
             pltpu.VMEM((coarse_cells, fine_cells), jnp.float32),
             pltpu.VMEM((fine_cells, coarse_cells), jnp.float32),
-            pltpu.SemaphoreType.DMA((5 * tiles,)),
-            pltpu.SemaphoreType.DMA((turns, MESSAGES)),
-            pltpu.SemaphoreType.DMA((turns, MESSAGES)),
+            pltpu.VMEM((7, zone_table.shape[0], ROWS, LANES), jnp.float32),
+            pltpu.VMEM((token_rows, LANES), jnp.float32),
+            pltpu.SemaphoreType.DMA((2, 5)),
+            pltpu.SemaphoreType.DMA((turns, ROUTES)),
+            pltpu.SemaphoreType.DMA((turns, ROUTES)),
         ],
         compiler_params=pltpu.CompilerParams(
             collective_id=0, has_side_effects=True, vmem_limit_bytes=KERNEL_BYTES
@@ -925,7 +942,7 @@
             scratch_shapes=[
                 pltpu.VMEM(sizes_of(peak_fine)[2], jnp.float32),
                 pltpu.VMEM(sizes_of(peak_coarse)[2], jnp.float32),
-                pltpu.SemaphoreType.DMA((5 * tiles,)),
+                pltpu.SemaphoreType.DMA((2, 4)),
             ],
             compiler_params=pltpu.CompilerParams(vmem_limit_bytes=KERNEL_BYTES),
             name="finish",

time: 40 us -> 34.5 us (0.86)
  Pallas kernels: 39.2 us -> 33.7 us
    pallas_call x1, Pallas kernels: 34.6 us -> 29.2 us  [on_device(): pl.pallas_call(waves_kernel, out_shape=state_of(peak_fine) + state_of(pea...]
where the time goes in v3:
time: 34.5 us; the launch traced here: 34.4 us
  Pallas kernels  33.7 us (98%)
  between operations  0.65 us (2%)
    pallas_call x1, Pallas kernels, on_device(): pl.pallas_call(waves_kernel, out_shape=state_of(peak_fine) + state_of(pea...  29.2 us
    pallas_call x1, Pallas kernels, on_device(): pl.pallas_call(finish_kernel, out_shape=[jax.ShapeDtypeStruct(array.shape...  4.52 us

profile of v3, /device:TPU:1, one launch (start us, length us, event | category | flops | bytes accessed | tf_op | source)
XLA Modules:
  0.0 34.4 jit_solution(6452202651637748200)
XLA Ops:
  0.6 29.2 %waves.1 = (f32[6,3,16,32,128]{4,3,2,1,0:T(8,128)S(1)}, f32[3,3,16,32,128]{4,3,2,1,0:T(8,128)S(1)}, f32[6,3,12,16,128]{4,3,2,1,0:T(8,128)S(1)}, f32[3,12,16,128]...) custom-call(f32[8,5]{1,0:T(8,128)} %refs_0_.1, ...), custom_call_target="tpu_custom_call" | custom-call | tf_op jit(solution)/shard_map/waves/pallas_call | solution.py:898
  29.8 4.5 %finish.1 = (f32[3,12,16,384]{3,2,1,0:T(8,128)}, f32[6,12,16,384]{3,2,1,0:T(8,128)}, f32[6,12,16,384]{3,2,1,0:T(8,128)}, f32[12,16,384]{2,1,0:T(8,128)}, f32[3,4...) custom-call(f32[6,3,16,32,128]{4,3,2,1,0:T(8,128)S(1)} %get-tuple-element.18., ...), custom_call_target="tpu_custom_call" | custom-call | tf_op jit(solution)/shard_map/finish/pallas_call | solution.py:937

commit v4 on v3

--- a/solution.py
+++ b/solution.py
@@ -26,7 +26,6 @@
 BUOYANCY, LAME, SHEAR, DECAY, DAMPING, VOLUMETRIC, SCALE = range(7)
 
 MESH = pl.DeviceIdType.MESH
-EXACT = lax.Precision.HIGHEST
 
 
 def property_tables(table_ref, spacing):
@@ -402,7 +401,7 @@
         share = interp_ref[1, phase].astype(jnp.float32) / 8.0
         matrix = jnp.where(fine == 3 * coarse + phase, share, matrix)
         matrix = jnp.where(fine == 3 * coarse - 3 + phase, 1.0 - share, matrix)
-    return matrix
+    return matrix.astype(jnp.bfloat16)
 
 
 def gather_matrix(restrict_ref, coarse_cells, fine_cells):
@@ -412,37 +411,53 @@
     for phase in range(3):
         weight = restrict_ref[1, phase].astype(jnp.float32)
         matrix = jnp.where(fine == 3 * coarse + phase, weight, matrix)
-    return matrix
+    return matrix.astype(jnp.bfloat16)
 
 
 def lift_matrix(interp_ref, fine_rows, rows):
-    target = lax.broadcasted_iota(jnp.int32, (2 * fine_rows, 2 * rows), 0)
-    source = lax.broadcasted_iota(jnp.int32, (2 * fine_rows, 2 * rows), 1)
-    matrix = jnp.zeros((2 * fine_rows, 2 * rows), jnp.float32)
+    shape = (2 * fine_rows, 6 * rows)
+    target = lax.broadcasted_iota(jnp.int32, shape, 0)
+    source = lax.broadcasted_iota(jnp.int32, shape, 1)
+    matrix = jnp.zeros(shape, jnp.float32)
     for phase in range(3):
         share = interp_ref[0, phase].astype(jnp.float32) / 8.0
-        for ghost in range(2):
-            for layer in range(2):
-                blend = (2.0 if ghost == layer else 1.0) / 3.0
-                for ahead in range(2):
-                    weight = (share if ahead == 0 else 1.0 - share) * blend
-                    base = 6 * (source - layer * rows - ahead) + 2 * phase + ghost
-                    inside = (source >= layer * rows + ahead) & (source < (layer + 1) * rows)
-                    matrix = jnp.where((target == base) & inside, weight, matrix)
-    return matrix
+        for begin in range(0, 6 * rows, rows):
+            ghost = begin // rows % 2
+            for ahead in range(2):
+                base = 6 * (source - begin - ahead) + 2 * phase + ghost
+                inside = (source >= begin + ahead) & (source < begin + rows)
+                weight = share if ahead == 0 else 1.0 - share
+                matrix = jnp.where((target == base) & inside, weight, matrix)
+    return matrix.astype(jnp.bfloat16)
+
+
+def three_parts(value):
+    parts = []
+    for _ in range(3):
+        part = value.astype(jnp.bfloat16)
+        value = value - part.astype(jnp.float32)
+        parts.append(part)
+    return jnp.concatenate(parts, axis=0)
+
+
+def exact_dot(left, right):
+    count = left.shape[0]
+    product = jnp.dot(three_parts(left), right, preferred_element_type=jnp.float32)
+    return product[:count] + (product[count : 2 * count] + product[2 * count :])
 
 
 class Coupling:
     def __init__(self, fine, coarse, interp_ref, restrict_ref, refs):
         self.fine, self.coarse = fine, coarse
         self.interp_ref, self.restrict_ref = interp_ref, restrict_ref
-        self.heads, self.lifted, self.layers, self.spread, self.gather = refs
+        self.heads, self.lifted, self.layers, self.spread, self.gather, self.lift = refs
         self.block = self.heads.shape[2] // 2
 
     def clear(self):
         coarse_cells, fine_cells = self.spread.shape
         self.spread[...] = spread_matrix(self.interp_ref, coarse_cells, fine_cells)
         self.gather[...] = gather_matrix(self.restrict_ref, coarse_cells, fine_cells)
+        self.lift[...] = lift_matrix(self.interp_ref, self.fine.rows, self.block)
 
     def restrict(self, turn, ref, along_z):
         fine, coarse = self.fine, self.coarse
@@ -459,9 +474,7 @@
                         for phase in range(3)
                     )
                     self.layers[begin : begin + ROWS, tile * LANES : (tile + 1) * LANES] = block
-        gathered = jnp.dot(
-            self.layers[...], self.gather[...], precision=EXACT, preferred_element_type=jnp.float32
-        )
+        gathered = exact_dot(self.layers[...], self.gather[...])
         gathered = gathered / jnp.full(gathered.shape, mass, jnp.float32)
         for slot in range(3):
             for row in range(coarse.rows):
@@ -474,17 +487,14 @@
 
     def interpolate(self, turn):
         fine = self.fine
-        lift = lift_matrix(self.interp_ref, fine.rows, self.block)
-        lifted = [
-            jnp.dot(lift, self.heads[turn, slot], precision=EXACT, preferred_element_type=jnp.float32)
-            for slot in range(3)
-        ]
-        ghosts = jnp.dot(
-            jnp.concatenate(lifted, axis=0),
-            self.spread[...],
-            precision=EXACT,
-            preferred_element_type=jnp.float32,
-        )
+        lifted = []
+        for slot in range(3):
+            first = self.heads[turn, slot, 0 : self.block, :]
+            second = self.heads[turn, slot, self.block : 2 * self.block, :]
+            layers = [(2.0 * first + second) / 3.0, (first + 2.0 * second) / 3.0]
+            parts = three_parts(jnp.concatenate(layers, axis=0))
+            lifted.append(jnp.dot(self.lift[...], parts, preferred_element_type=jnp.float32))
+        ghosts = exact_dot(jnp.concatenate(lifted, axis=0), self.spread[...])
         for slot in range(3):
             for row in range(fine.rows):
                 begin = 2 * (slot * fine.rows + row)
@@ -506,11 +516,12 @@
             "head": (lat, self.depths - 1, top, bottom),
             "corner": (lat - 1, self.depths - 1, top & has_previous, bottom & has_next),
             "lift": (lat, 0, bottom, top),
-            "next": (lat + 1, depth, has_next, has_previous),
-            "previous": (lat - 1, depth, has_previous, has_next),
-            "down": (lat, depth + 1, has_lower, has_upper),
-            "up": (lat, depth - 1, has_upper, has_lower),
         }
+        for grid in ("fine", "coarse"):
+            self.routes[f"next {grid}"] = (lat + 1, depth, has_next, has_previous)
+            self.routes[f"previous {grid}"] = (lat - 1, depth, has_previous, has_next)
+            self.routes[f"down {grid}"] = (lat, depth + 1, has_lower, has_upper)
+            self.routes[f"up {grid}"] = (lat, depth - 1, has_upper, has_lower)
         self.top, self.bottom = top, bottom
 
     def target(self, route):
@@ -576,29 +587,29 @@
                 coupling.lifted.at[turn, slot, :, :, pl.ds(ROWS - low, low), :],
                 coarse.around_z.at[turn, slot, :, :, pl.ds(ROWS - low, low), :],
             )
-        for grid in (fine, coarse):
+        for name, grid in (("fine", fine), ("coarse", coarse)):
             ref = grid.velocity if velocity else grid.stress
             inner = pl.ds(ROWS, grid.depth)
             for slot, (part, (low, high)) in enumerate(along_x):
                 self.add(
-                    "next",
+                    f"next {name}",
                     ref.at[part, :, pl.ds(2 + grid.rows - low, low), inner, :],
                     grid.below_x.at[turn, slot, :, pl.ds(2 - low, low), :, :],
                 )
                 self.add(
-                    "previous",
+                    f"previous {name}",
                     ref.at[part, :, pl.ds(2, high), inner, :],
                     grid.above_x.at[turn, slot, :, pl.ds(0, high), :, :],
                 )
             for slot, (part, (low, high)) in enumerate(along_z):
                 rows = pl.ds(2, grid.rows)
                 self.add(
-                    "down",
+                    f"down {name}",
                     ref.at[part, :, rows, pl.ds(ROWS + grid.depth - low, low), :],
                     grid.around_z.at[turn, slot, :, :, pl.ds(ROWS - low, low), :],
                 )
                 self.add(
-                    "up",
+                    f"up {name}",
                     ref.at[part, :, rows, pl.ds(ROWS, high), :],
                     grid.around_z.at[turn, slot, :, :, pl.ds(2 * ROWS, high), :],
                 )
@@ -643,7 +654,8 @@
                 self.settle(route, self.send_sems.at[self.numbers[route]])
 
 
-ROUTES = 7
+ROUTES = 11
+EDGE = 2
 KERNEL_BYTES = 32 * 1024 * 1024
 
 
@@ -660,7 +672,7 @@
     states = [take(5), take(5)]
     fine = Field(1.0, states[0] + take(4))
     coarse = Field(3.0, states[1] + take(4))
-    coupling = Coupling(fine, coarse, interp_ref, restrict_ref, take(5))
+    coupling = Coupling(fine, coarse, interp_ref, restrict_ref, take(6))
     filled, token = take(2)
     load_sems, send_sems, recv_sems = take(3)
     place = Place()
@@ -722,33 +734,61 @@
 
         turns[turn].send("lift")
 
-    def open_turn(turn):
-        turns[turn].send("head", "corner", "next", "previous", "down", "up")
+    def open_coarse(turn):
+        turns[turn].send(
+            "head", "corner", "next coarse", "previous coarse", "down coarse", "up coarse"
+        )
+
+    def open_fine(turn):
+        turns[turn].send("next fine", "previous fine", "down fine", "up fine")
+
+    def outer_z(grid, turn):
+        if turn % 2 == 1:
+            grid.stress_outer_z(turn)
+        else:
+            grid.velocity_outer_z(turn)
+
+    def outer_x(grid, turn):
+        if turn % 2 == 1:
+            grid.stress_outer_x(turn)
+        else:
+            grid.velocity_outer_x(turn)
 
     def close_turn(turn):
+        last = turn == 2 * STEPS - 1
+        turns[turn].receive("down coarse", "up coarse", "lift")
+        outer_z(coarse, turn)
+        turns[turn].receive("next coarse", "previous coarse")
+        outer_x(coarse, turn)
+        if last:
+            coarse.each_row(coarse.raise_peak)
+        else:
+            open_coarse(turn + 1)
         turns[turn].receive("head", "corner")
 
         @pl.when(place.bottom)
         def _():
             coupling.interpolate(turn)
 
-        turns[turn].receive("down", "up", "lift")
-        for grid in grids:
-            if turn % 2 == 1:
-                grid.stress_outer_z(turn)
-            else:
-                grid.velocity_outer_z(turn)
-        turns[turn].receive("next", "previous")
-        for grid in grids:
-            if turn % 2 == 1:
-                grid.stress_outer_x(turn)
-            else:
-                grid.velocity_outer_x(turn)
+        turns[turn].receive("down fine", "up fine")
+        outer_z(fine, turn)
+        if last:
+            fine.each_row(fine.raise_peak, EDGE, fine.rows - EDGE)
+        turns[turn].receive("next fine", "previous fine")
+        outer_x(fine, turn)
+        if not last:
+            open_fine(turn + 1)
+            restrict(turn + 1)
 
     finish("stress")
     pl.semaphore_wait(barrier, peers)
-    open_turn(0)
-    coupling.clear()
+    open_coarse(0)
+    open_fine(0)
+
+    @pl.when(place.bottom)
+    def _():
+        coupling.clear()
+
     restrict(0)
 
     for grid in grids:
@@ -773,6 +813,7 @@
     for grid in grids:
         grid.fill_props(table_ref, filled)
 
+    early = 2 * fine.rows // 3
     for step in range(STEPS):
         turn = 2 * step
         if step == 0:
@@ -782,29 +823,24 @@
         for grid in grids:
             grid.each_row(grid.velocity_inner)
         if step > 0:
-            fine.each_row(fine.raise_peak, 0, fine.rows // 2)
+            fine.each_row(fine.raise_peak, 0, early)
         close_turn(turn)
-        open_turn(turn + 1)
-        restrict(turn + 1)
         if step == 0:
             finish("memory")
             finish("peak")
         else:
-            fine.each_row(fine.raise_peak, fine.rows // 2)
+            fine.each_row(fine.raise_peak, early)
             coarse.each_row(coarse.raise_peak)
         turns[turn].sent()
         for grid in grids:
             grid.each_row(grid.stress_inner)
         close_turn(turn + 1)
-        if step < STEPS - 1:
-            open_turn(turn + 2)
-            restrict(turn + 2)
     turns[2 * STEPS - 1].sent()
 
 
 def finish_kernel(*refs):
     states, outputs = [refs[0:5], refs[5:10]], [refs[10:14], refs[14:18]]
-    peaks, sems = refs[18:20], refs[20]
+    raised_fine, sems = refs[18:20]
     wholes = []
     for grid, ((stress, velocity, memory, peak, _), arrays) in enumerate(zip(states, outputs)):
         new_velocity, new_stress, new_memory, _ = arrays
@@ -823,10 +859,20 @@
                 pltpu.make_async_copy(source, place, sems.at[grid, index]).start()
         wholes += [(array, sems.at[grid, index]) for index, array in enumerate(arrays)]
     for grid, ((stress, _, _, peak, props), (_, _, _, new_peak), raised) in enumerate(
-        zip(states, outputs, peaks)
+        zip(states, outputs, (raised_fine, None))
     ):
         tiles, rows, depth, _ = peak.shape
-        half = rows // 2
+
+        def emit(source, begin, end, new_peak=new_peak, grid=grid, tiles=tiles):
+            span = pl.ds(begin, end - begin)
+            for tile in range(tiles):
+                place = new_peak.at[span, :, pl.ds(tile * LANES, LANES)]
+                pltpu.make_async_copy(source.at[tile, span], place, sems.at[grid, 3]).start()
+
+        if raised is None:
+            emit(peak, 0, rows)
+            continue
+        emit(peak, EDGE, rows - EDGE)
 
         def body(row, carry):
             for tile in range(tiles):
@@ -838,12 +884,9 @@
                 raised[tile, row] = jnp.maximum(peak[tile, row], strain)
             return carry
 
-        for begin, end in ((0, half), (half, rows)):
+        for begin, end in ((0, EDGE), (rows - EDGE, rows)):
             lax.fori_loop(begin, end, body, 0)
-            span = pl.ds(begin, end - begin)
-            for tile in range(tiles):
-                place = new_peak.at[span, :, pl.ds(tile * LANES, LANES)]
-                pltpu.make_async_copy(raised.at[tile, span], place, sems.at[grid, 3]).start()
+            emit(raised, begin, end)
     for array, sem in wholes:
         pltpu.make_async_copy(array, array, sem).wait()
 
@@ -906,8 +949,9 @@
             pltpu.VMEM((turns, 3, 2 * block, coarse_cells), jnp.float32),
             pltpu.VMEM((turns, 3, coarse_cells // LANES, coarse_rows, ROWS, LANES), jnp.float32),
             pltpu.VMEM((3 * coarse_rows * ROWS, fine_cells), jnp.float32),
-            pltpu.VMEM((coarse_cells, fine_cells), jnp.float32),
-            pltpu.VMEM((fine_cells, coarse_cells), jnp.float32),
+            pltpu.VMEM((coarse_cells, fine_cells), jnp.bfloat16),
+            pltpu.VMEM((fine_cells, coarse_cells), jnp.bfloat16),
+            pltpu.VMEM((2 * fine_rows, 6 * block), jnp.bfloat16),
             pltpu.VMEM((7, zone_table.shape[0], ROWS, LANES), jnp.float32),
             pltpu.VMEM((token_rows, LANES), jnp.float32),
             pltpu.SemaphoreType.DMA((2, 5)),
@@ -941,7 +985,6 @@
             out_specs=[hbm] * 8,
             scratch_shapes=[
                 pltpu.VMEM(sizes_of(peak_fine)[2], jnp.float32),
-                pltpu.VMEM(sizes_of(peak_coarse)[2], jnp.float32),
                 pltpu.SemaphoreType.DMA((2, 4)),
             ],
             compiler_params=pltpu.CompilerParams(vmem_limit_bytes=KERNEL_BYTES),

time: 34.5 us -> 33.3 us (0.965)
  Pallas kernels: 33.7 us -> 32.5 us
    pallas_call x1, Pallas kernels: 4.52 us -> 2.55 us  [on_device(): pl.pallas_call(finish_kernel, out_shape=[jax.ShapeDtypeStruct(array.shape...]
    pallas_call x1, Pallas kernels: 29.2 us -> 29.9 us  [on_device(): pl.pallas_call(waves_kernel, out_shape=state_of(peak_fine) + state_of(pea...]
where the time goes in v4:
time: 33.3 us; the launch traced here: 33.1 us
  Pallas kernels  32.5 us (98%)
  between operations  0.65 us (2%)
    pallas_call x1, Pallas kernels, on_device(): pl.pallas_call(waves_kernel, out_shape=state_of(peak_fine) + state_of(pea...  29.9 us
    pallas_call x1, Pallas kernels, on_device(): pl.pallas_call(finish_kernel, out_shape=[jax.ShapeDtypeStruct(array.shape...  2.55 us

profile of v4, /device:TPU:1, one launch (start us, length us, event | category | flops | bytes accessed | tf_op | source)
XLA Modules:
  0.0 33.1 jit_solution(9231199789674845369)
XLA Ops:
  0.6 29.9 %waves.1 = (f32[6,3,16,32,128]{4,3,2,1,0:T(8,128)S(1)}, f32[3,3,16,32,128]{4,3,2,1,0:T(8,128)S(1)}, f32[6,3,12,16,128]{4,3,2,1,0:T(8,128)S(1)}, f32[3,12,16,128]...) custom-call(f32[8,5]{1,0:T(8,128)} %refs_0_.1, ...), custom_call_target="tpu_custom_call" | custom-call | tf_op jit(solution)/shard_map/waves/pallas_call | solution.py:941
  30.6 2.6 %finish.1 = (f32[3,12,16,384]{3,2,1,0:T(8,128)}, f32[6,12,16,384]{3,2,1,0:T(8,128)}, f32[6,12,16,384]{3,2,1,0:T(8,128)}, f32[12,16,384]{2,1,0:T(8,128)}, f32[3,4...) custom-call(f32[6,3,16,32,128]{4,3,2,1,0:T(8,128)S(1)} %get-tuple-element.18., ...), custom_call_target="tpu_custom_call" | custom-call | tf_op jit(solution)/shard_map/finish/pallas_call | solution.py:981

commit v5 on v4

--- a/solution.py
+++ b/solution.py
@@ -154,6 +154,16 @@
     def along_y(self, ref, part, row, kind):
         tiles = [self.cells(ref, part, tile, row) for tile in range(self.tiles)]
         return difference_y(tiles, kind)
+
+    def each_pair(self, body):
+        def step(pair, carry):
+            body(2 * pair)
+            body(2 * pair + 1)
+            return carry
+
+        lax.fori_loop(0, self.rows // 2, step, 0)
+        if self.rows % 2 == 1:
+            body(self.rows - 1)
 
     def each_row(self, body, begin=0, end=None):
         def step(row, carry):
@@ -297,7 +307,7 @@
                         buoyancy = self.props[BUOYANCY, tile, row, pl.ds(begin, ROWS), :]
                         place[...] = place[...] + buoyancy * term
 
-        self.each_row(body)
+        self.each_pair(body)
 
     def stress_inner(self, row):
         velocity, stress, memory = self.velocity, self.stress, self.memory
@@ -381,7 +391,7 @@
                     )
                     self.add_rates(rates, tile, row, begin, ROWS)
 
-        self.each_row(body)
+        self.each_pair(body)
 
     def raise_peak(self, row):
         for tile in range(self.tiles):
@@ -821,7 +831,7 @@
         else:
             turns[turn - 1].sent()
         for grid in grids:
-            grid.each_row(grid.velocity_inner)
+            grid.each_pair(grid.velocity_inner)
         if step > 0:
             fine.each_row(fine.raise_peak, 0, early)
         close_turn(turn)
@@ -833,7 +843,7 @@
             coarse.each_row(coarse.raise_peak)
         turns[turn].sent()
         for grid in grids:
-            grid.each_row(grid.stress_inner)
+            grid.each_pair(grid.stress_inner)
         close_turn(turn + 1)
     turns[2 * STEPS - 1].sent()
 

time: 33.3 us -> 32.9 us (0.988); the launches traced: 33.1 us -> 32.4 us
  Pallas kernels: 32.5 us -> 31.8 us
    pallas_call x1, Pallas kernels: 29.9 us -> 29.2 us  [on_device(): pl.pallas_call(waves_kernel, out_shape=state_of(peak_fine) + state_of(pea...]
where the time goes in v5:
time: 32.9 us; the launch traced here: 32.4 us
  Pallas kernels  31.8 us (97%)
  between operations  0.65 us (2%)
    pallas_call x1, Pallas kernels, on_device(): pl.pallas_call(waves_kernel, out_shape=state_of(peak_fine) + state_of(pea...  29.2 us
    pallas_call x1, Pallas kernels, on_device(): pl.pallas_call(finish_kernel, out_shape=[jax.ShapeDtypeStruct(array.shape...  2.55 us

profile of v5, /device:TPU:1, one launch (start us, length us, event | category | flops | bytes accessed | tf_op | source)
XLA Modules:
  0.0 32.4 jit_solution(13038707614361894860)
XLA Ops:
  0.6 29.2 %waves.1 = (f32[6,3,16,32,128]{4,3,2,1,0:T(8,128)S(1)}, f32[3,3,16,32,128]{4,3,2,1,0:T(8,128)S(1)}, f32[6,3,12,16,128]{4,3,2,1,0:T(8,128)S(1)}, f32[3,12,16,128]...) custom-call(f32[8,5]{1,0:T(8,128)} %refs_0_.1, ...), custom_call_target="tpu_custom_call" | custom-call | tf_op jit(solution)/shard_map/waves/pallas_call | solution.py:951
  29.8 2.6 %finish.1 = (f32[3,12,16,384]{3,2,1,0:T(8,128)}, f32[6,12,16,384]{3,2,1,0:T(8,128)}, f32[6,12,16,384]{3,2,1,0:T(8,128)}, f32[12,16,384]{2,1,0:T(8,128)}, f32[3,4...) custom-call(f32[6,3,16,32,128]{4,3,2,1,0:T(8,128)S(1)} %get-tuple-element.18., ...), custom_call_target="tpu_custom_call" | custom-call | tf_op jit(solution)/shard_map/finish/pallas_call | solution.py:991
